TPU v7x, 8 devices: a whole 2x2x1 slice. The times are simulated.
8 devices in a mesh: ep: 8 (over z, y, x, core).
Axes of the slice: x: 2, y: 2, z: 1, core: 2. Of those that a mesh axis runs over, the one named last changes fastest.
Arguments:
- tokens: bfloat16 [1024, 4096], P('ep')
- k_cache: bfloat16 [1024, 64, 32, 128], P('ep')
- v_cache: bfloat16 [1024, 64, 32, 128], P('ep')
- positions: int32 [1024], P('ep')
- expert_one: int32 [1024], P('ep')
- expert_two: int32 [1024], P('ep')
- eligible: int32 [1024, 8], P('ep')
- ln1_gain: bfloat16 [4096], replicated
- ln1_bias: bfloat16 [4096], replicated
- w_query: bfloat16 [4096, 4096], replicated
- b_query: bfloat16 [4096], replicated
- w_key: bfloat16 [4096, 4096], replicated
- b_key: bfloat16 [4096], replicated
- w_value: bfloat16 [4096, 4096], replicated
- b_value: bfloat16 [4096], replicated
- w_out: bfloat16 [4096, 4096], replicated
- b_out: bfloat16 [4096], replicated
- ln2_gain: bfloat16 [4096], replicated
- ln2_bias: bfloat16 [4096], replicated
- w_router: bfloat16 [4096, 8], replicated
- w_gate: bfloat16 [8, 4096, 1376], P('ep')
- w_up: bfloat16 [8, 4096, 1376], P('ep')
- w_down: bfloat16 [8, 1376, 4096], P('ep')
Outputs:
- output 1: bfloat16 [1024, 4096], P('ep')
- output 2: bfloat16 [1024, 32, 128], P('ep')
- output 3: bfloat16 [1024, 32, 128], P('ep')
All inputs are finite; a program needn't handle non-finite values.
Results may differ from a plain program's by a relative error of at most 0.0102763.
Values are sent between devices in bfloat16 or wider.
A program may use at most 1.25 GiB of HBM per device.

v0:
```python
import jax
import jax.numpy as jnp
from jax import lax
from jax.sharding import PartitionSpec as P

ROPE_BASE = 10000.0
LN_EPS = 1e-5


def layer_norm(values_in, gain, bias):
    mean_val = jnp.mean(values_in, axis=-1, keepdims=True)
    centered = values_in - mean_val
    var_val = jnp.mean(centered * centered, axis=-1, keepdims=True)
    return centered * lax.rsqrt(var_val + LN_EPS) * gain.astype(jnp.float32) + bias.astype(jnp.float32)


def rope_tables(positions, head_dim):
    half_dim = head_dim // 2
    inv_freq = ROPE_BASE ** (jnp.arange(half_dim, dtype=jnp.float32) * (-2.0 / head_dim))
    angles = positions.astype(jnp.float32)[:, None] * inv_freq[None, :]
    angles = jnp.concatenate([angles, angles], axis=-1)
    return jnp.cos(angles), jnp.sin(angles)


def apply_rope(values_in, cos_tab, sin_tab):
    half_dim = values_in.shape[-1] // 2
    rotated = jnp.concatenate([-values_in[..., half_dim:], values_in[..., :half_dim]], axis=-1)
    return values_in * cos_tab[:, None, :] + rotated * sin_tab[:, None, :]


def attention_block(tokens, k_cache, v_cache, positions, ln1_gain, ln1_bias, w_query, b_query, w_key, b_key, w_value, b_value, w_out, b_out):
    tok_count, seq_len, kv_heads, head_dim = k_cache.shape
    num_heads = w_query.shape[1] // head_dim
    group_size = num_heads // kv_heads
    x_f = tokens.astype(jnp.float32)
    h_one = layer_norm(x_f, ln1_gain, ln1_bias).astype(jnp.bfloat16)
    cos_tab, sin_tab = rope_tables(positions, head_dim)
    q_lin = jnp.dot(h_one, w_query, preferred_element_type=jnp.float32) + b_query.astype(jnp.float32)
    q_rot = apply_rope(q_lin.reshape(tok_count, num_heads, head_dim), cos_tab, sin_tab).astype(jnp.bfloat16)
    q_grp = q_rot.reshape(tok_count, kv_heads, group_size, head_dim)
    k_lin = jnp.dot(h_one, w_key, preferred_element_type=jnp.float32) + b_key.astype(jnp.float32)
    key_new = apply_rope(k_lin.reshape(tok_count, kv_heads, head_dim), cos_tab, sin_tab).astype(jnp.bfloat16)
    v_lin = jnp.dot(h_one, w_value, preferred_element_type=jnp.float32) + b_value.astype(jnp.float32)
    value_new = v_lin.astype(jnp.bfloat16).reshape(tok_count, kv_heads, head_dim)
    score_scale = head_dim ** -0.5
    s_cache = jnp.einsum('tkgd,tskd->tkgs', q_grp, k_cache, preferred_element_type=jnp.float32) * score_scale
    valid_mask = jnp.arange(seq_len)[None, None, None, :] < positions[:, None, None, None]
    s_cache = jnp.where(valid_mask, s_cache, -jnp.inf)
    s_new = jnp.einsum('tkgd,tkd->tkg', q_grp, key_new, preferred_element_type=jnp.float32) * score_scale
    top_val = jnp.maximum(jnp.max(s_cache, axis=-1), s_new)
    e_cache = jnp.exp(s_cache - top_val[..., None])
    e_new = jnp.exp(s_new - top_val)
    denom_sum = jnp.sum(e_cache, axis=-1) + e_new
    p_cache = (e_cache / denom_sum[..., None]).astype(jnp.bfloat16)
    p_new = (e_new / denom_sum).astype(jnp.bfloat16)
    attn_vals = jnp.einsum('tkgs,tskd->tkgd', p_cache, v_cache, preferred_element_type=jnp.float32)
    attn_vals = attn_vals + p_new.astype(jnp.float32)[..., None] * value_new.astype(jnp.float32)[:, :, None, :]
    attn_flat = attn_vals.astype(jnp.bfloat16).reshape(tok_count, num_heads * head_dim)
    x_mid = (x_f + jnp.dot(attn_flat, w_out, preferred_element_type=jnp.float32) + b_out.astype(jnp.float32)).astype(jnp.bfloat16)
    return x_mid, key_new, value_new


def router_gates(h_two, w_router, expert_one, expert_two, eligible):
    logits = jnp.dot(h_two, w_router, preferred_element_type=jnp.float32)
    expert_ids = jnp.arange(logits.shape[1])[None, :]
    hit_one = expert_ids == expert_one[:, None]
    hit_two = expert_ids == expert_two[:, None]
    keep_one = eligible == 1
    keep_two = keep_one & jnp.logical_not(hit_one)
    prob_one = jax.nn.softmax(jnp.where(keep_one, logits, -jnp.inf), axis=-1)
    prob_two = jax.nn.softmax(jnp.where(keep_two, logits, -jnp.inf), axis=-1)
    gate_one = jnp.sum(jnp.where(hit_one, prob_one, 0.0), axis=-1)
    gate_two = jnp.sum(jnp.where(hit_two, prob_two, 0.0), axis=-1)
    return gate_one, gate_two


def send_plan(expert_one, expert_two, local_experts, groups, tok_count):
    num_experts = local_experts * groups
    pair_expert = jnp.concatenate([expert_one, expert_two])
    token_ids = jnp.arange(tok_count, dtype=jnp.int32)
    pair_token = jnp.concatenate([token_ids, token_ids])
    one_hot = (pair_expert[:, None] == jnp.arange(num_experts, dtype=jnp.int32)[None, :]).astype(jnp.int32)
    pair_slot = jnp.sum(one_hot * jnp.cumsum(one_hot, axis=0), axis=1) - 1
    buffer_row = ((pair_expert % local_experts) * groups + pair_expert // local_experts) * tok_count + pair_slot
    src_token = jax.ops.segment_sum(pair_token, buffer_row, num_segments=num_experts * tok_count)
    return buffer_row, src_token


def expert_mlp(expert_in, w_gate, w_up, w_down):
    u_val = jnp.einsum('emd,edf->emf', expert_in, w_gate, preferred_element_type=jnp.float32)
    v_val = jnp.einsum('emd,edf->emf', expert_in, w_up, preferred_element_type=jnp.float32)
    z_val = (jax.nn.silu(u_val) * v_val).astype(jnp.bfloat16)
    return jnp.einsum('emf,efd->emd', z_val, w_down, preferred_element_type=jnp.float32).astype(jnp.bfloat16)


def solution(mesh):
    groups = mesh.shape['ep']

    def local_step(tokens, k_cache, v_cache, positions, expert_one, expert_two, eligible, ln1_gain, ln1_bias, w_query, b_query, w_key, b_key, w_value, b_value, w_out, b_out, ln2_gain, ln2_bias, w_router, w_gate, w_up, w_down):
        x_mid, key_new, value_new = attention_block(tokens, k_cache, v_cache, positions, ln1_gain, ln1_bias, w_query, b_query, w_key, b_key, w_value, b_value, w_out, b_out)
        h_two = layer_norm(x_mid.astype(jnp.float32), ln2_gain, ln2_bias).astype(jnp.bfloat16)
        gate_one, gate_two = router_gates(h_two, w_router, expert_one, expert_two, eligible)
        tok_count, d_model = h_two.shape
        local_experts = w_gate.shape[0]
        num_experts = local_experts * groups
        buffer_row, src_token = send_plan(expert_one, expert_two, local_experts, groups, tok_count)
        send_rows = jnp.take(h_two, src_token, axis=0).reshape(local_experts, groups, tok_count, d_model)
        recv_rows = lax.all_to_all(send_rows, 'ep', 1, 1, tiled=True)
        expert_in = recv_rows.reshape(local_experts, groups * tok_count, d_model)
        expert_out = expert_mlp(expert_in, w_gate, w_up, w_down)
        back_rows = lax.all_to_all(expert_out.reshape(local_experts, groups, tok_count, d_model), 'ep', 1, 1, tiled=True)
        back_flat = back_rows.reshape(num_experts * tok_count, d_model)
        out_one = jnp.take(back_flat, buffer_row[:tok_count], axis=0)
        out_two = jnp.take(back_flat, buffer_row[tok_count:], axis=0)
        y_sum = gate_one[:, None] * out_one.astype(jnp.float32) + gate_two[:, None] * out_two.astype(jnp.float32)
        tokens_out = (x_mid.astype(jnp.float32) + y_sum).astype(jnp.bfloat16)
        return tokens_out, key_new, value_new

    row_spec = P('ep', None)
    cache_spec = P('ep', None, None, None)
    vec_spec = P('ep')
    rep_one = P(None)
    rep_two = P(None, None)
    expert_spec = P('ep', None, None)
    in_specs = (row_spec, cache_spec, cache_spec, vec_spec, vec_spec, vec_spec, row_spec, rep_one, rep_one, rep_two, rep_one, rep_two, rep_one, rep_two, rep_one, rep_two, rep_one, rep_one, rep_one, rep_two, expert_spec, expert_spec, expert_spec)
    out_specs = (row_spec, expert_spec, expert_spec)
    return jax.shard_map(local_step, mesh=mesh, in_specs=in_specs, out_specs=out_specs, check_vma=False)
```

profile of v0, /device:TPU:0, one launch (start us, length us, event | category | flops | bytes accessed | tf_op | source)
XLA Modules:
  0.0 448.0 jit_solution(17142841296311507584)
XLA Ops:
  5.7 2.3 scatter_custom_fusion
  9.5 1.7 fusion.21
  11.2 13.0 %fusion.31 = f32[16,8,32,128]{3,1,2,0:T(8,128)S(1)} fusion(bf16[4096,4096]{1,0:T(8,128)(2,1)} %param.34, f32[4096]{0:T(1024)S(1)} %convert_element_type.100, bf16[128,4096]{1,0:T(8,128)(2,1)S(1)} %copy-done.1, f32[4096]{0:T(1024)S(1)} %convert_element_type.98, f32[4096]{0:T(1024)S(1)} %convert_element_type.97, f32[128]{0:T(128)S(1)} %add_rsqrt_fusion.1, ...), kind=kOutput, calls=%fused_computation.48 | convolution fusion | flops 4298637312 | bytes 36750336 | tf_op jit(solution)/shard_map/dot_general | solution.py:38
  24.9 13.0 %fusion.32 = f32[16,8,32,128]{3,1,2,0:T(8,128)S(1)} fusion(bf16[4096,4096]{1,0:T(8,128)(2,1)} %param.36, f32[4096]{0:T(1024)S(1)} %convert_element_type.103, bf16[128,4096]{1,0:T(8,128)(2,1)S(1)} %copy-done.1, f32[4096]{0:T(1024)S(1)} %convert_element_type.98, f32[4096]{0:T(1024)S(1)} %convert_element_type.97, f32[128]{0:T(128)S(1)} %add_rsqrt_fusion.1, ...), kind=kOutput, calls=%fused_computation.49 | convolution fusion | flops 4298637312 | bytes 36750336 | tf_op jit(solution)/shard_map/dot_general | solution.py:41
  40.3 1.7 fusion.28
  43.0 41.1 %fusion.2 = f32[128,32,1,64]{3,2,1,0:T(1,128)} fusion(bf16[128,64,32,128]{3,2,1,0:T(8,128)(2,1)} %param.26, bf16[128,32,128,1]{2,1,0,3:T(8,128)(2,1)S(1)} %bitcast.86), kind=kOutput, calls=%fused_computation.6 | convolution fusion | flops 67108864 | bytes 69206016 | tf_op jit(solution)/shard_map/tkgd,tskd->tkgs/dot_general | solution.py:46
  84.1 4.7 %copy.33 = f32[128,32,1,64]{0,3,1,2:T(8,128)S(1)} copy(f32[128,32,1,64]{3,2,1,0:T(1,128)} %fusion.2) | data formatting | bytes 2097152 | tf_op jit(solution)/shard_map/tkgd,tskd->tkgs/dot_general | solution.py:46
  88.8 1.8 fusion.29
  91.5 3.9 copy.38
  95.5 15.1 %fusion.33 = bf16[16,8,32,128]{3,1,2,0:T(8,128)(2,1)S(1)} fusion(bf16[4096,4096]{1,0:T(8,128)(2,1)} %param.38, f32[4096]{0:T(1024)S(1)} %convert_element_type.108, bf16[128,4096]{1,0:T(8,128)(2,1)S(1)} %copy-done.1, f32[4096]{0:T(1024)S(1)} %convert_element_type.98, f32[4096]{0:T(1024)S(1)} %convert_element_type.97, f32[128]{0:T(128)S(1)} %add_rsqrt_fusion.1, ...), kind=kOutput, calls=%fused_computation.50 | convolution fusion | flops 4299161600 | bytes 35701760 | tf_op jit(solution)/shard_map/dot_general | solution.py:43
  111.4 42.2 %fusion = f32[128,32,1,128]{3,2,1,0:T(1,128)} fusion(bf16[128,32,64,1]{2,3,1,0:T(2,128)(2,1)} %copy.38, bf16[128,64,32,128]{3,2,1,0:T(8,128)(2,1)} %param.27), kind=kOutput, calls=%fused_computation.4 | convolution fusion | flops 67108864 | bytes 69730304 | tf_op jit(solution)/shard_map/tkgs,tskd->tkgd/dot_general | solution.py:56
  153.6 1.9 add_convert_fusion.2
  155.5 13.6 %fusion.60 = (f32[128]{0:T(128)S(1)}, f32[128,4096]{1,0:T(8,128)S(1)}) fusion(f32[4096]{0:T(1024)S(1)} %convert_element_type.112, bf16[4096,4096]{1,0:T(8,128)(2,1)} %param.40, bf16[16,8,32,128]{3,2,1,0:T(8,128)(2,1)S(1)} %bitcast.85, bf16[128,4096]{1,0:T(8,128)(2,1)S(1)} %copy-done.1), kind=kOutput, calls=%fused_computation.114 | convolution fusion | flops 4298113024 | bytes 37765632 | tf_op jit(solution)/shard_map/dot_general | solution.py:59
  170.3 7.7 %gather_fusion = bf16[1024,4096]{1,0:T(8,128)(2,1)} fusion(bf16[128,4096]{1,0:T(8,128)(2,1)S(1)} %add_convert_fusion.1, s32[1024]{0:T(1024)S(1)} %fusion.51), kind=kCustom, calls=%fused_computation.2 | custom fusion | bytes 16781312 | tf_op jit(solution)/shard_map/jit(_take)/gather | solution.py:107
  178.0 7.4 %broadcast_select_fusion = bf16[1,8,128,4096]{3,2,0,1:T(8,128)(2,1)} fusion(bf16[1,8,128,4096]{3,2,0,1:T(8,128)(2,1)} %bitcast.79, pred[8,128]{1,0:T(8,128)(4,1)S(1)} %and_bitcast_fusion), kind=kLoop, calls=%fused_computation.14 | loop fusion | flops 4194304 | bytes 16778240 | tf_op jit(solution)/shard_map/jit(_take)/select_n | solution.py:107
  185.4 98.1 %all_to_all.10 = bf16[1,8,128,4096]{3,2,0,1:T(8,128)(2,1)S(1)} all-to-all(bf16[1,8,128,4096]{3,2,0,1:T(8,128)(2,1)} %broadcast_select_fusion), channel_id=1, replica_groups=mesh['ep'=8] {'ep'}, dimensions={1} | all-to-all | bytes 16777216 | tf_op jit(solution)/shard_map/all_to_all | solution.py:108
  283.5 14.7 %fusion.6 = f32[1024,1376]{0,1:T(8,128)S(1)} fusion(bf16[1024,4096]{1,0:T(8,128)(2,1)S(1)} %bitcast.83, bf16[1,4096,1376]{1,2,0:T(8,128)(2,1)} %param.46), kind=kOutput, calls=%fused_computation.10 | convolution fusion | flops 11542724608 | bytes 25296896 | tf_op jit(solution)/shard_map/emd,edf->emf/dot_general | solution.py:91
  298.2 15.4 %multiply_convert_fusion = bf16[1024,1376]{0,1:T(8,128)(2,1)S(1)} fusion(f32[1024,1376]{0,1:T(8,128)S(1)} %fusion.6, bf16[1024,4096]{1,0:T(8,128)(2,1)S(1)} %bitcast.84, bf16[1,4096,1376]{1,2,0:T(8,128)(2,1)} %param.45), kind=kOutput, calls=%fused_computation.16 | convolution fusion | flops 11551178752 | bytes 28114944 | tf_op jit(solution)/shard_map/emd,edf->emf/dot_general | solution.py:90
  313.6 18.5 %fusion.10 = bf16[1024,4096]{1,0:T(8,128)(2,1)} fusion(bf16[1024,1376]{0,1:T(8,128)(2,1)S(1)} %multiply_convert_fusion, bf16[1,1376,4096]{2,1,0:T(8,128)(2,1)} %param.47), kind=kOutput, calls=%fused_computation.15 | convolution fusion | flops 11546918912 | bytes 22478848 | tf_op jit(solution)/shard_map/emf,efd->emd/dot_general | solution.py:93
  332.1 4.1 all-to-all-start.1
  336.8 93.4 %all-to-all-done.1 = bf16[1,8,128,4096]{3,2,0,1:T(8,128)(2,1)} async-done(((bf16[1,8,128,4096]{3,2,0,1:T(8,128)(2,1)}), bf16[1,8,128,4096]{3,2,0,1:T(8,128)(2,1)}, u32[]{:S(2)}, u32[]{:S(2)}) %all-to-all-start.1) | async-done | bytes 8388640 | tf_op jit(solution)/shard_map/all_to_all | solution.py:111
  430.2 6.7 %gather_fusion.1 = bf16[128,4096]{1,0:T(8,128)(2,1)S(1)} fusion(bf16[1024,4096]{1,0:T(8,128)(2,1)} %bitcast.21, s32[1024]{0:T(1024)S(1)} %get-tuple-element.34), kind=kCustom, calls=%fused_computation.clone | custom fusion | bytes 2097664 | tf_op jit(solution)/shard_map/jit(_take)/gather | solution.py:113
  436.9 7.6 %gather_fusion.2 = bf16[128,4096]{1,0:T(8,128)(2,1)} fusion(bf16[1024,4096]{1,0:T(8,128)(2,1)} %bitcast.21, s32[1024]{0:T(1024)S(1)} %get-tuple-element.33), kind=kCustom, calls=%fused_computation.1.clone | custom fusion | bytes 2097664 | tf_op jit(solution)/shard_map/jit(_take)/gather | solution.py:114
  444.5 3.0 add_convert_fusion
  (86 shorter events, 13.7 us)
Async XLA Ops:
  0.6 335.7 %copy-start = (bf16[4096,8]{0,1:T(8,128)(2,1)S(1)}, bf16[4096,8]{0,1:T(8,128)(2,1)}, u32[]{:S(2)}) copy-start(bf16[4096,8]{0,1:T(8,128)(2,1)} %param.44) | copy-start | bytes 196612
  0.6 10.5 %copy-start.1 = (bf16[128,4096]{1,0:T(8,128)(2,1)S(1)}, bf16[128,4096]{1,0:T(8,128)(2,1)}, u32[]{:S(2)}) copy-start(bf16[128,4096]{1,0:T(8,128)(2,1)} %param.25) | copy-start | bytes 3145732
  0.7 10.5 %copy-start.5 = (bf16[4096]{0:T(1024)(128)(2,1)S(1)}, bf16[4096]{0:T(1024)(128)(2,1)}, u32[]{:S(2)}) copy-start(bf16[4096]{0:T(1024)(128)(2,1)} %param.32) | copy-start | bytes 24580
  0.7 10.5 %copy-start.6 = (bf16[4096]{0:T(1024)(128)(2,1)S(1)}, bf16[4096]{0:T(1024)(128)(2,1)}, u32[]{:S(2)}) copy-start(bf16[4096]{0:T(1024)(128)(2,1)} %param.33) | copy-start | bytes 24580
  0.7 10.5 %copy-start.7 = (bf16[4096]{0:T(1024)(128)(2,1)S(1)}, bf16[4096]{0:T(1024)(128)(2,1)}, u32[]{:S(2)}) copy-start(bf16[4096]{0:T(1024)(128)(2,1)} %param.35) | copy-start | bytes 24580
  24.2 0.7 copy-start.8
  42.0 1.0 copy-start.3
  42.0 46.8 %copy-start.2 = (bf16[128,32,128]{2,1,0:T(8,128)(2,1)}, bf16[128,32,128]{2,1,0:T(8,128)(2,1)S(1)}, u32[]{:S(2)}) copy-start(bf16[128,32,128]{2,1,0:T(8,128)(2,1)S(1)} %get-tuple-element.18) | copy-start | bytes 3145732
  91.2 4.3 copy-start.9
  110.7 0.7 copy-start.10
  111.4 42.2 %copy-start.4 = (bf16[16,8,32,128]{3,2,1,0:T(8,128)(2,1)}, bf16[16,8,32,128]{3,2,1,0:T(8,128)(2,1)S(1)}, u32[]{:S(2)}) copy-start(bf16[16,8,32,128]{3,2,1,0:T(8,128)(2,1)S(1)} %copy.44) | copy-start | bytes 3145732
  169.1 0.7 copy-start.11
  169.1 0.7 copy-start.12
  332.1 4.1 copy-start.15
  332.1 4.2 copy-start.14
  332.1 4.6 %copy-start.13 = (s32[128]{0:T(128)S(1)}, s32[128]{0:T(128)}, u32[]{:S(2)}) copy-start(s32[128]{0:T(128)} %param.29) | copy-start | bytes 1540
  332.1 4.6 %copy-start.16 = (s32[128]{0:T(128)S(1)}, s32[128]{0:T(128)}, u32[]{:S(2)}) copy-start(s32[128]{0:T(128)} %param.30) | copy-start | bytes 1540
  332.1 98.1 %all-to-all-start.1 = ((bf16[1,8,128,4096]{3,2,0,1:T(8,128)(2,1)}), bf16[1,8,128,4096]{3,2,0,1:T(8,128)(2,1)}, u32[]{:S(2)}, u32[]{:S(2)}) async-start(bf16[1,8,128,4096]{3,2,0,1:T(8,128)(2,1)} %bitcast.82), calls=%async_computation.1 | async-start | bytes 16777216 | tf_op jit(solution)/shard_map/all_to_all | solution.py:111
where the time goes:
time: 457 us; the launch traced here: 448 us
  matrix products  187 us (41%)
  blocking collectives  98.1 us (21%)
  waiting for transfers between devices  93.4 us (20%)
  local copies, waits for them, and re-layouts  35.4 us (8%)
  other arithmetic  28.4 us (6%)
    all_to_all x1, blocking collectives, local_step(): recv_rows = lax.all_to_all(send_rows, 'ep', 1, 1, tiled=True)  98.1 us
    all_to_all x1, waiting for transfers between devices, local_step(): lax.all_to_all(expert_out.reshape(local_experts, groups, tok_count, d_mod...  93.4 us
    dot_general x1, matrix products, attention_block(): jnp.einsum('tkgs,tskd->tkgd', p_cache, v_cache, preferred_element_type=jn...  42.2 us
    dot_general x1, matrix products, attention_block(): jnp.einsum('tkgd,tskd->tkgs', q_grp, k_cache, preferred_element_type=jnp....  41.1 us
    dot_general x1, matrix products, expert_mlp(): jnp.einsum('emf,efd->emd', z_val, w_down, preferred_element_type=jnp.floa...  18.5 us
    dot_general x1, matrix products, expert_mlp(): jnp.einsum('emd,edf->emf', expert_in, w_gate, preferred_element_type=jnp....  15.4 us
    dot_general x1, matrix products, attention_block(): jnp.dot(h_one, w_value, preferred_element_type=jnp.float32)  15.1 us
    dot_general x1, matrix products, expert_mlp(): jnp.einsum('emd,edf->emf', expert_in, w_up, preferred_element_type=jnp.fl...  14.7 us
  transfers between devices with their start and end apart: 1, of which 1 were waited for; matrix products, arithmetic and copies ran while one was open for 0% of the time, Pallas kernels for 0%

commit v1 on v0

v1 whole, which is shorter than its diff:
```python
import functools

import jax
import jax.numpy as jnp
from jax import lax
from jax.experimental import pallas as pl
from jax.experimental.pallas import tpu as pltpu
from jax.sharding import PartitionSpec as P

ROPE_BASE = 10000.0
LN_EPS = 1e-5
VMEM_CAP = 60 * 1024 * 1024
F32 = jnp.float32
BF16 = jnp.bfloat16


def layer_norm(values_in, gain, bias):
    mean_val = jnp.mean(values_in, axis=-1, keepdims=True)
    centered = values_in - mean_val
    var_val = jnp.mean(centered * centered, axis=-1, keepdims=True)
    return centered * lax.rsqrt(var_val + LN_EPS) * gain.astype(F32) + bias.astype(F32)


def rope_tables(positions, head_dim):
    half_dim = head_dim // 2
    inv_freq = ROPE_BASE ** (jnp.arange(half_dim, dtype=F32) * (-2.0 / head_dim))
    angles = positions.astype(F32)[:, None] * inv_freq[None, :]
    cos_half, sin_half = jnp.cos(angles), jnp.sin(angles)
    return jnp.concatenate([cos_half, cos_half], axis=-1), jnp.concatenate([-sin_half, sin_half], axis=-1)


def qkv_kernel(heads, x_ref, gain_ref, bias_ref, cos_ref, sin_ref, wq_ref, wk_ref, wv_ref, bq_ref, bk_ref, bv_ref,
               q_out, k_out, v_out, h_scr, q_scr, k_scr, v_scr):
    step = pl.program_id(0)
    toks = x_ref.shape[0]
    hd = cos_ref.shape[1]

    @pl.when(step == 0)
    def _():
        h_scr[...] = layer_norm(x_ref[...].astype(F32), gain_ref[...], bias_ref[...]).astype(BF16)

    h_one = h_scr[...]
    per_step = wq_ref.shape[1] // hd
    for w_ref, b_ref, scr, rotate in ((wq_ref, bq_ref, q_scr, True), (wk_ref, bk_ref, k_scr, True), (wv_ref, bv_ref, v_scr, False)):
        lin = jnp.dot(h_one, w_ref[...], preferred_element_type=F32) + b_ref[...].astype(F32)
        for sub in range(per_step):
            part = lin[:, sub * hd:(sub + 1) * hd]
            if rotate:
                part = part * cos_ref[...] + pltpu.roll(part, hd // 2, 1) * sin_ref[...]
            scr[pl.ds(step * per_step + sub, toks, stride=heads), :] = part

    @pl.when(step == pl.num_programs(0) - 1)
    def _():
        for scr, out in ((q_scr, q_out), (k_scr, k_out), (v_scr, v_out)):
            out[...] = scr[...].astype(BF16)


def qkv_project(tokens, gain, bias, cos_tab, sin_tab, wq, bq, wk, bk, wv, bv):
    toks, d_model = tokens.shape
    hd = cos_tab.shape[1]
    heads = wq.shape[1] // hd
    tile = 256
    full = lambda shape: pl.BlockSpec(shape, lambda i: (0,) * len(shape))
    w_spec = pl.BlockSpec((d_model, tile), lambda i: (0, i))
    b_spec = pl.BlockSpec((1, tile), lambda i: (0, i))
    out = jax.ShapeDtypeStruct((toks * heads, hd), BF16)
    row = lambda v: v.reshape(1, -1)
    return pl.pallas_call(
        functools.partial(qkv_kernel, heads),
        grid=(wq.shape[1] // tile,),
        in_specs=[full((toks, d_model)), full((1, d_model)), full((1, d_model)), full((toks, hd)), full((toks, hd)),
                  w_spec, w_spec, w_spec, b_spec, b_spec, b_spec],
        out_specs=[full((toks * heads, hd))] * 3,
        out_shape=[out] * 3,
        scratch_shapes=[pltpu.VMEM((toks, d_model), BF16)] + [pltpu.VMEM((toks * heads, hd), F32)] * 3,
        compiler_params=pltpu.CompilerParams(dimension_semantics=("arbitrary",), vmem_limit_bytes=VMEM_CAP),
        cost_estimate=pl.CostEstimate(flops=6 * toks * d_model * wq.shape[1], bytes_accessed=6 * d_model * wq.shape[1], transcendentals=0),
        name="qkv_project",
    )(tokens, row(gain), row(bias), cos_tab, sin_tab, wq, wk, wv, row(bq), row(bk), row(bv))


def attend_kernel(pos_ref, q_ref, kn_ref, vn_ref, k_ref, v_ref, o_ref):
    blk, seq, heads, hd = k_ref.shape
    groups = 128 // heads
    scale = hd ** -0.5
    rows = seq // groups
    two = 2 * heads
    r_id = lax.broadcasted_iota(jnp.int32, (two, 128), 0)
    l_id = lax.broadcasted_iota(jnp.int32, (two, 128), 1)
    pick = (l_id // two == r_id // heads) & (l_id % heads == r_id % heads)
    diag = lax.broadcasted_iota(jnp.int32, (heads, 128), 1) % heads == lax.broadcasted_iota(jnp.int32, (heads, 128), 0)
    s_id = groups * lax.broadcasted_iota(jnp.int32, (rows, 128), 0) + lax.broadcasted_iota(jnp.int32, (rows, 128), 1) // heads
    zero_q = jnp.zeros((heads, hd), BF16)

    def all_groups(vals, op):
        vals = op(vals, pltpu.roll(vals, heads, 1))
        return op(vals, pltpu.roll(vals, 2 * heads, 1))

    for tok in range(blk):
        pos = pos_ref[pl.program_id(0) * blk + tok]
        q_tok = q_ref[tok]
        top = jnp.concatenate([q_tok, zero_q], axis=1)
        bot = jnp.concatenate([zero_q, q_tok], axis=1)
        q_mat = jnp.concatenate([top, bot, top, bot], axis=0)
        k_tok = k_ref[tok].reshape(seq // 2, 2, heads, hd)
        k_mat = jnp.concatenate([k_tok[:, 0].reshape(seq // 2 * heads, hd), k_tok[:, 1].reshape(seq // 2 * heads, hd)], axis=1)
        raw = lax.dot_general(k_mat, q_mat, (((1,), (1,)), ((), ())), preferred_element_type=F32)
        s_cache = jnp.sum(jnp.where(pick[None], raw.reshape(rows, two, 128), 0.0), axis=1) * scale
        s_cache = jnp.where(s_id < pos, s_cache, -jnp.inf)
        new_col = jnp.sum(q_tok.astype(F32) * kn_ref[tok].astype(F32), axis=1, keepdims=True)
        s_new = jnp.sum(jnp.where(diag, new_col, 0.0), axis=0, keepdims=True) * scale
        top_val = jnp.maximum(all_groups(jnp.max(s_cache, axis=0, keepdims=True), jnp.maximum), s_new)
        e_cache = jnp.exp(s_cache - top_val)
        e_new = jnp.exp(s_new - top_val)
        denom = all_groups(jnp.sum(e_cache, axis=0, keepdims=True), jnp.add) + e_new
        p_cache = e_cache / denom
        p_new = (e_new / denom).astype(BF16).astype(F32)
        p_mat = jnp.concatenate([jnp.where(diag, p_cache[r:r + 1, :], 0.0).astype(BF16) for r in range(rows)], axis=1)
        vals = jnp.dot(p_mat, v_ref[tok].reshape(seq * heads, hd), preferred_element_type=F32)
        p_col = jnp.sum(jnp.where(diag, p_new, 0.0), axis=1, keepdims=True) * (1.0 / groups)
        o_ref[tok] = vals + p_col * vn_ref[tok].astype(F32)


def attend(positions, q_rot, key_new, value_new, k_cache, v_cache):
    toks, seq, heads, hd = k_cache.shape
    blk = 4
    row = pl.BlockSpec((blk, heads, hd), lambda i, pos: (i, 0, 0))
    cache = pl.BlockSpec((blk, seq, heads, hd), lambda i, pos: (i, 0, 0, 0))
    return pl.pallas_call(
        attend_kernel,
        grid_spec=pltpu.PrefetchScalarGridSpec(
            num_scalar_prefetch=1, grid=(toks // blk,),
            in_specs=[row, row, row, cache, cache], out_specs=row),
        out_shape=jax.ShapeDtypeStruct((toks, heads, hd), F32),
        compiler_params=pltpu.CompilerParams(dimension_semantics=("arbitrary",), vmem_limit_bytes=VMEM_CAP),
        cost_estimate=pl.CostEstimate(flops=4 * toks * seq * heads * hd * 32, bytes_accessed=4 * toks * seq * heads * hd, transcendentals=0),
        name="attend",
    )(positions, q_rot, key_new, value_new, k_cache, v_cache)


def out_kernel(heads, x_ref, a_ref, w_ref, b_ref, gain_ref, bias_ref, wr_ref, e1_ref, e2_ref, el_ref,
               x1_out, h2_out, g_out, a_scr):
    step = pl.program_id(0)
    toks = x_ref.shape[0]
    hd = a_ref.shape[1]
    tile = w_ref.shape[1]

    @pl.when(step == 0)
    def _():
        for head in range(heads):
            a_scr[:, head * hd:(head + 1) * hd] = a_ref[pl.ds(head, toks, stride=heads), :].astype(BF16)

    cols = pl.ds(pl.multiple_of(step * tile, tile), tile)
    lin = jnp.dot(a_scr[...], w_ref[...], preferred_element_type=F32)
    x1_out[:, cols] = (x_ref[:, cols].astype(F32) + lin + b_ref[...].astype(F32)).astype(BF16)

    @pl.when(step == pl.num_programs(0) - 1)
    def _():
        h_two = layer_norm(x1_out[...].astype(F32), gain_ref[...], bias_ref[...]).astype(BF16)
        h2_out[...] = h_two
        logits = jnp.dot(h_two, wr_ref[...], preferred_element_type=F32)
        ids = lax.broadcasted_iota(jnp.int32, logits.shape, 1)
        hit_one, hit_two = ids == e1_ref[...], ids == e2_ref[...]
        keep_one = el_ref[...] == 1
        keep_two = keep_one & jnp.logical_not(hit_one)

        def prob(keep):
            masked = jnp.where(keep, logits, -jnp.inf)
            expd = jnp.exp(masked - jnp.max(masked, axis=1, keepdims=True))
            return expd / jnp.sum(expd, axis=1, keepdims=True)

        g_out[...] = jnp.where(hit_one, prob(keep_one), 0.0) + jnp.where(hit_two, prob(keep_two), 0.0)


def out_project(tokens, attn, w_out, b_out, gain, bias, w_router, e1, e2, eligible):
    toks, d_model = tokens.shape
    rows, hd = attn.shape
    tile = 256
    experts = w_router.shape[1]
    full = lambda shape: pl.BlockSpec(shape, lambda i: (0,) * len(shape))
    row = lambda v: v.reshape(1, -1)
    return pl.pallas_call(
        functools.partial(out_kernel, rows // toks),
        grid=(d_model // tile,),
        in_specs=[full((toks, d_model)), full((rows, hd)), pl.BlockSpec((w_out.shape[0], tile), lambda i: (0, i)),
                  pl.BlockSpec((1, tile), lambda i: (0, i)), full((1, d_model)), full((1, d_model)), full((d_model, experts)),
                  full((toks, 1)), full((toks, 1)), full((toks, experts))],
        out_specs=[full((toks, d_model)), full((toks, d_model)), full((toks, experts))],
        out_shape=[jax.ShapeDtypeStruct((toks, d_model), BF16), jax.ShapeDtypeStruct((toks, d_model), BF16),
                   jax.ShapeDtypeStruct((toks, experts), F32)],
        scratch_shapes=[pltpu.VMEM((toks, w_out.shape[0]), BF16)],
        compiler_params=pltpu.CompilerParams(dimension_semantics=("arbitrary",), vmem_limit_bytes=VMEM_CAP),
        cost_estimate=pl.CostEstimate(flops=2 * toks * d_model * d_model, bytes_accessed=2 * d_model * d_model, transcendentals=0),
        name="out_project",
    )(tokens, attn, w_out, row(b_out), row(gain), row(bias), w_router, e1[:, None], e2[:, None], eligible)


def expert_mlp(expert_in, w_gate, w_up, w_down):
    u_val = jnp.dot(expert_in, w_gate, preferred_element_type=F32)
    v_val = jnp.dot(expert_in, w_up, preferred_element_type=F32)
    z_val = (jax.nn.silu(u_val) * v_val).astype(BF16)
    return jnp.dot(z_val, w_down, preferred_element_type=F32).astype(BF16)


def solution(mesh):
    def local_step(tokens, k_cache, v_cache, positions, expert_one, expert_two, eligible, ln1_gain, ln1_bias, w_query, b_query, w_key, b_key, w_value, b_value, w_out, b_out, ln2_gain, ln2_bias, w_router, w_gate, w_up, w_down):
        toks, seq, heads, hd = k_cache.shape
        cos_tab, sin_tab = rope_tables(positions, hd)
        q_rot, key_new, value_new = (
            v.reshape(toks, heads, hd)
            for v in qkv_project(tokens, ln1_gain, ln1_bias, cos_tab, sin_tab, w_query, b_query, w_key, b_key, w_value, b_value))
        attn = attend(positions, q_rot, key_new, value_new, k_cache, v_cache)
        x_mid, h_two, gates = out_project(tokens, attn.reshape(toks * heads, hd), w_out, b_out, ln2_gain, ln2_bias, w_router, expert_one, expert_two, eligible)
        me = lax.axis_index('ep')
        gates_all = lax.all_gather(gates, 'ep', axis=0, tiled=True)
        h_all = lax.all_gather(h_two, 'ep', axis=0, tiled=True)
        mine = jnp.arange(gates.shape[1])[None, :] == me
        weight = jnp.sum(jnp.where(mine, gates_all, 0.0), axis=1, keepdims=True)
        expert_out = expert_mlp(h_all, w_gate[0], w_up[0], w_down[0])
        part = (weight * expert_out.astype(F32)).astype(BF16)
        y_sum = lax.psum_scatter(part, 'ep', scatter_dimension=0, tiled=True)
        tokens_out = (x_mid.astype(F32) + y_sum.astype(F32)).astype(BF16)
        return tokens_out, key_new, value_new

    row_spec = P('ep', None)
    cache_spec = P('ep', None, None, None)
    vec_spec = P('ep')
    rep_one = P(None)
    rep_two = P(None, None)
    expert_spec = P('ep', None, None)
    in_specs = (row_spec, cache_spec, cache_spec, vec_spec, vec_spec, vec_spec, row_spec, rep_one, rep_one, rep_two, rep_one, rep_two, rep_one, rep_two, rep_one, rep_two, rep_one, rep_one, rep_one, rep_two, expert_spec, expert_spec, expert_spec)
    out_specs = (row_spec, expert_spec, expert_spec)
    return jax.shard_map(local_step, mesh=mesh, in_specs=in_specs, out_specs=out_specs, check_vma=False)
```

time: 457 us -> 368 us (0.81); the launches traced: 448 us -> 367 us
  Pallas kernels: 0 us -> 163 us
  matrix products: 187 us -> 52.6 us
  blocking collectives: 98.1 us -> 18.5 us
  other arithmetic: 28.4 us -> 4.38 us
  local copies, waits for them, and re-layouts: 35.4 us -> 16.8 us
  between operations: 1.54 us -> 14.1 us
    pallas_call x0 -> x3, Pallas kernels: none -> 163 us  [the longest x1 99.2 us: attend(): pl.pallas_call(attend_kernel, grid_spec=pltpu.PrefetchScalarGridSpec(num_...]
    dot_general x10 -> x3, matrix products: 187 us -> 52.6 us  [the longest x1 18.4 us: expert_mlp(): v_val = jnp.dot(expert_in, w_up, preferred_element_type=F32)]
    all_to_all x1 -> x0, blocking collectives: 98.1 us -> none  [local_step(): recv_rows = lax.all_to_all(send_rows, 'ep', 1, 1, tiled=True)]
    all_to_all x1 -> x0, waiting for transfers between devices: 93.4 us -> none  [local_step(): lax.all_to_all(expert_out.reshape(local_experts, groups, tok_count, d_mod...]
    reduce_scatter x0 -> x1, waiting for transfers between devices: none -> 62.4 us  [local_step(): y_sum = lax.psum_scatter(part, 'ep', scatter_dimension=0, tiled=True)]
    all_gather x0 -> x1, waiting for transfers between devices: none -> 34.8 us  [local_step(): h_all = lax.all_gather(h_two, 'ep', axis=0, tiled=True)]
    gather x3 -> x0, local copies, waits for them, and re-layouts: 22 us -> none  [the longest x1 7.74 us: local_step(): jnp.take(h_two, src_token, axis=0)]
    all_gather x0 -> x1, blocking collectives: none -> 18.5 us  [local_step(): gates_all = lax.all_gather(gates, 'ep', axis=0, tiled=True)]
  transfers between devices with their start and end apart: 1 -> 2, of which waited for: 1 -> 2; matrix products, arithmetic and copies ran while one was open for 0% -> 0% of each run, Pallas kernels for 0% -> 0%
where the time goes in v1:
time: 368 us; the launch traced here: 367 us
  Pallas kernels  163 us (44%)
  waiting for transfers between devices  97.2 us (26%)
  matrix products  52.6 us (14%)
  blocking collectives  18.5 us (5%)
  local copies, waits for them, and re-layouts  16.8 us (5%)
  between operations  14.1 us (4%)
  other arithmetic  4.38 us (1%)
    pallas_call x1, Pallas kernels, attend(): pl.pallas_call(attend_kernel, grid_spec=pltpu.PrefetchScalarGridSpec(num_...  99.2 us
    reduce_scatter x1, waiting for transfers between devices, local_step(): y_sum = lax.psum_scatter(part, 'ep', scatter_dimension=0, tiled=True)  62.4 us
    pallas_call x1, Pallas kernels, qkv_project(): pl.pallas_call(functools.partial(qkv_kernel, heads), grid=(wq.shape[1] //...  40.2 us
    all_gather x1, waiting for transfers between devices, local_step(): h_all = lax.all_gather(h_two, 'ep', axis=0, tiled=True)  34.8 us
    pallas_call x1, Pallas kernels, out_project(): pl.pallas_call(functools.partial(out_kernel, rows // toks), grid=(d_model...  23.7 us
    all_gather x1, blocking collectives, local_step(): gates_all = lax.all_gather(gates, 'ep', axis=0, tiled=True)  18.5 us
    dot_general x1, matrix products, expert_mlp(): v_val = jnp.dot(expert_in, w_up, preferred_element_type=F32)  18.4 us
    dot_general x1, matrix products, expert_mlp(): u_val = jnp.dot(expert_in, w_gate, preferred_element_type=F32)  18.4 us
  transfers between devices with their start and end apart: 2, of which 2 were waited for; matrix products, arithmetic and copies ran while one was open for 0% of the time, Pallas kernels for 0%

profile of v1, /device:TPU:0, one launch (start us, length us, event | category | flops | bytes accessed | tf_op | source)
XLA Modules:
  0.0 366.7 jit_solution(15208856094044525278)
XLA Ops:
  7.2 0.7 convert_element_type.24
  7.9 1.3 reshape.54.gain_ref
  9.2 1.3 reshape.55.bias_ref
  10.5 1.3 reshape.56.bq_ref
  11.8 1.3 reshape.57.bk_ref
  13.1 1.3 reshape.58.bv_ref
  14.4 1.3 reshape.63.b_ref
  15.7 1.3 reshape.64.gain_ref
  17.0 1.3 reshape.65.bias_ref
  18.3 1.4 copy.27.e1_ref
  19.7 1.4 copy.28.e2_ref
  21.1 1.4 copy.29.el_ref
  22.5 2.2 copy.26.wr_ref
  25.0 0.7 pad_maximum_fusion
  25.7 40.2 %qkv_project.1 = (bf16[4096,128]{1,0:T(8,128)(2,1)}, bf16[4096,128]{1,0:T(8,128)(2,1)}, bf16[4096,128]{1,0:T(8,128)(2,1)}) custom-call(bf16[128,4096]{1,0:T(8,128)(2,1)} %x_ref.3, bf16[1,4096]{1,0:T(2,128)(2,1)} %reshape.54.gain_ref, bf16[1,4096]{1,0:T(2,128)(2,1)} %reshape.55.bias_ref, f32[128,128]{1,0:T(8,128)} %get-tuple-element.18.cos_ref, ...), custom_call_target="tpu_custom_call" | custom-call | flops 12884901888 | bytes 100663296 | tf_op jit(solution)/shard_map/qkv_project/pallas_call | solution.py:68
  65.9 99.2 %attend.1 = f32[128,32,128]{2,1,0:T(8,128)} custom-call(s32[128]{0:T(128)} %pos_ref.1, bf16[128,32,128]{2,1,0:T(8,128)(2,1)} %bitcast.27, bf16[128,32,128]{2,1,0:T(8,128)(2,1)} %bitcast.23, bf16[128,32,128]{2,1,0:T(8,128)(2,1)} %bitcast.25, bf16[128,64,32,128]{3,2,1,0:T(8,128)(2,1)} %k_ref.1, bf16[128,64,32,128]{3,2,1,0:T(8,128)(2,1)} %v_ref.1), custom_call_target="tpu_custom_call" | custom-call | flops 4294967296 | bytes 134217728 | tf_op jit(solution)/shard_map/attend/pallas_call | solution.py:129
  165.1 23.7 %out_project.1 = (bf16[128,4096]{1,0:T(8,128)(2,1)}, bf16[128,4096]{1,0:T(8,128)(2,1)}, f32[128,8]{1,0:T(8,128)}) custom-call(bf16[128,4096]{1,0:T(8,128)(2,1)} %x_ref.3, f32[4096,128]{1,0:T(8,128)} %bitcast.22, bf16[4096,4096]{1,0:T(8,128)(2,1)} %w_ref.1, bf16[1,4096]{1,0:T(2,128)(2,1)} %reshape.63.b_ref, bf16[1,4096]{1,0:T(2,128)(2,1)} %reshape.64.gain_ref, ...), custom_call_target="tpu_custom_call" | custom-call | flops 4294967296 | bytes 33554432 | tf_op jit(solution)/shard_map/out_project/pallas_call | solution.py:182
  188.9 18.5 %all_gather.6 = f32[1024,8]{1,0:T(8,128)S(1)} all-gather(f32[128,8]{1,0:T(8,128)} %get-tuple-element.13), channel_id=1, replica_groups=mesh['ep'=8] {'ep'}, dimensions={0}, use_global_device_ids=true | all-gather | bytes 36864 | tf_op jit(solution)/shard_map/all_gather | solution.py:215
  207.6 34.8 %all-gather.2.cloned.1.call-done = bf16[1024,4096]{1,0:T(8,128)(2,1)} async-done(((bf16[128,4096]{1,0:T(8,128)(2,1)}), bf16[1024,4096]{1,0:T(8,128)(2,1)}) %all-gather.2.cloned.1.call-update) | async-done | bytes 8388624 | tf_op jit(solution)/shard_map/all_gather | solution.py:216
  242.4 18.4 %fusion.2 = f32[1024,1376]{0,1:T(8,128)} fusion(bf16[1024,4096]{1,0:T(8,128)(2,1)} %all-gather.2.cloned.1.call-done, bf16[1,4096,1376]{1,2,0:T(8,128)(2,1)} %param.44), kind=kOutput, calls=%fused_computation.3 | convolution fusion | flops 11542724608 | bytes 25296896 | tf_op jit(solution)/shard_map/dot_general | solution.py:200
  260.8 18.4 %multiply_convert_fusion.1 = bf16[1024,1376]{0,1:T(8,128)(2,1)S(1)} fusion(f32[1024,1376]{0,1:T(8,128)} %fusion.2, bf16[1024,4096]{1,0:T(8,128)(2,1)} %all-gather.2.cloned.1.call-done, bf16[1,4096,1376]{1,2,0:T(8,128)(2,1)} %param.43), kind=kOutput, calls=%fused_computation.7 | convolution fusion | flops 11551178752 | bytes 28114944 | tf_op jit(solution)/shard_map/dot_general | solution.py:199
  279.2 15.8 %multiply_convert_fusion = bf16[1024,4096]{1,0:T(8,128)(2,1)} fusion(f32[1024]{0:T(1024)S(1)} %select_reduce_fusion, bf16[1024,1376]{0,1:T(8,128)(2,1)S(1)} %multiply_convert_fusion.1, bf16[1,1376,4096]{2,1,0:T(8,128)(2,1)S(1)} %bitcast.31), kind=kOutput, calls=%fused_computation | convolution fusion | flops 11559501824 | bytes 22482944 | tf_op jit(solution)/shard_map/dot_general | solution.py:202
  295.1 62.4 %reduce-scatter.2.cloned.1.call-done = bf16[128,4096]{1,0:T(8,128)(2,1)} async-done(((bf16[1024,4096]{1,0:T(8,128)(2,1)}), bf16[128,4096]{1,0:T(8,128)(2,1)}) %reduce-scatter.2.cloned.1.call-update) | async-done | bytes 1048592 | tf_op jit(solution)/shard_map/reduce_scatter | solution.py:221
  357.5 2.4 add_convert_fusion
  (17 shorter events, 0.7 us)
Async XLA Ops:
  7.2 235.2 %all-gather.2.cloned.1.call-start = ((), (), s32[]{:S(2)}) async-start(), calls=%async_computation.1 | async-start | bytes 9437184 | tf_op jit(solution)/shard_map/all_gather | solution.py:216
  188.9 168.6 %reduce-scatter.2.cloned.1.call-start = ((), (), s32[]{:S(2)}) async-start(), calls=%async_computation.2 | async-start | bytes 9437184 | tf_op jit(solution)/shard_map/reduce_scatter | solution.py:221
  242.4 36.8 %slice-start = ((s8[11272192]{0:T(1024)(128)(4,1)}), s8[4194304]{0:T(1024)(128)(4,1)S(1)}, s32[]{:S(2)}) async-start(s8[11272192]{0:T(1024)(128)(4,1)} %bitcast.30), calls=%async_computation.3 | async-start | bytes 8388608
  242.4 36.8 %slice-start.1 = ((s8[11272192]{0:T(1024)(128)(4,1)}), s8[4194304]{0:T(1024)(128)(4,1)S(1)}, s32[]{:S(2)}) async-start(s8[11272192]{0:T(1024)(128)(4,1)} %bitcast.30), calls=%async_computation.4 | async-start | bytes 8388608
  260.8 18.4 %slice-start.2 = ((s8[11272192]{0:T(1024)(128)(4,1)}), s8[2883584]{0:T(1024)(128)(4,1)S(1)}, s32[]{:S(2)}) async-start(s8[11272192]{0:T(1024)(128)(4,1)} %bitcast.30), calls=%async_computation.5 | async-start | bytes 5767168
  295.1 62.4 %copy-start = (bf16[128,4096]{1,0:T(8,128)(2,1)S(1)}, bf16[128,4096]{1,0:T(8,128)(2,1)}, u32[]{:S(2)}) copy-start(bf16[128,4096]{1,0:T(8,128)(2,1)} %get-tuple-element.12) | copy-start | bytes 3145732
Sparse Core Ops, SparseCore 0:
  189.0 53.3 all-gather.1
  295.2 62.2 reduce-scatter.1

commit v2 on v1

v2 whole, which is shorter than its diff:
```python
import functools

import jax
import jax.numpy as jnp
from jax import lax
from jax.experimental import pallas as pl
from jax.experimental.pallas import tpu as pltpu
from jax.sharding import PartitionSpec as P

ROPE_BASE = 10000.0
LN_EPS = 1e-5
VMEM_CAP = 60 * 1024 * 1024
F32 = jnp.float32
BF16 = jnp.bfloat16


def layer_norm(values_in, gain, bias):
    mean_val = jnp.mean(values_in, axis=-1, keepdims=True)
    centered = values_in - mean_val
    var_val = jnp.mean(centered * centered, axis=-1, keepdims=True)
    return centered * lax.rsqrt(var_val + LN_EPS) * gain.astype(F32) + bias.astype(F32)


def rope_tables(positions, head_dim):
    half_dim = head_dim // 2
    inv_freq = ROPE_BASE ** (jnp.arange(half_dim, dtype=F32) * (-2.0 / head_dim))
    angles = positions.astype(F32)[:, None] * inv_freq[None, :]
    cos_half, sin_half = jnp.cos(angles), jnp.sin(angles)
    return jnp.concatenate([cos_half, cos_half], axis=-1), jnp.concatenate([-sin_half, sin_half], axis=-1)


def qkv_kernel(heads, x_ref, vec_ref, cos_ref, sin_ref, wq_ref, wk_ref, wv_ref, q_out, k_out, v_out, h_scr, q_scr, k_scr, v_scr):
    step = pl.program_id(0)
    toks = x_ref.shape[0]
    hd = cos_ref.shape[1]
    tile = wq_ref.shape[1]

    @pl.when(step == 0)
    def _():
        h_scr[...] = layer_norm(x_ref[...].astype(F32), vec_ref[0:1, :], vec_ref[1:2, :]).astype(BF16)

    h_one = h_scr[...]
    cols = pl.ds(pl.multiple_of(step * tile, tile), tile)
    per_step = tile // hd
    for row, w_ref, scr in ((2, wq_ref, q_scr), (3, wk_ref, k_scr), (4, wv_ref, v_scr)):
        lin = jnp.dot(h_one, w_ref[...], preferred_element_type=F32) + vec_ref[row:row + 1, cols]
        for sub in range(per_step):
            part = lin[:, sub * hd:(sub + 1) * hd]
            if row < 4:
                part = part * cos_ref[...] + pltpu.roll(part, hd // 2, 1) * sin_ref[...]
            scr[pl.ds(step * per_step + sub, toks, stride=heads), :] = part

    @pl.when(step == pl.num_programs(0) - 1)
    def _():
        for scr, out in ((q_scr, q_out), (k_scr, k_out), (v_scr, v_out)):
            out[...] = scr[...].astype(BF16)


def full_spec(shape):
    return pl.BlockSpec(shape, lambda *ids: (0,) * len(shape))


def qkv_project(tokens, vecs, cos_tab, sin_tab, wq, wk, wv):
    toks, d_model = tokens.shape
    hd = cos_tab.shape[1]
    heads = wq.shape[1] // hd
    tile = 512
    w_spec = pl.BlockSpec((d_model, tile), lambda i: (0, i))
    out = jax.ShapeDtypeStruct((toks * heads, hd), BF16)
    return pl.pallas_call(
        functools.partial(qkv_kernel, heads),
        grid=(wq.shape[1] // tile,),
        in_specs=[full_spec((toks, d_model)), full_spec(vecs.shape), full_spec((toks, hd)), full_spec((toks, hd)), w_spec, w_spec, w_spec],
        out_specs=[full_spec((toks * heads, hd))] * 3,
        out_shape=[out] * 3,
        scratch_shapes=[pltpu.VMEM((toks, d_model), BF16)] + [pltpu.VMEM((toks * heads, hd), F32)] * 3,
        compiler_params=pltpu.CompilerParams(dimension_semantics=("arbitrary",), vmem_limit_bytes=VMEM_CAP),
        cost_estimate=pl.CostEstimate(flops=6 * toks * d_model * wq.shape[1], bytes_accessed=6 * d_model * wq.shape[1], transcendentals=0),
        name="qkv_project",
    )(tokens, vecs, cos_tab, sin_tab, wq, wk, wv)


def attend_kernel(pos_ref, q_ref, kn_ref, vn_ref, k_ref, v_ref, o_ref):
    blk, seq, heads, hd = k_ref.shape
    groups = 128 // heads
    scale = hd ** -0.5
    rows = seq // groups
    half = rows // 2
    two = 2 * heads
    r_id = lax.broadcasted_iota(jnp.int32, (two, 128), 0)
    l_id = lax.broadcasted_iota(jnp.int32, (two, 128), 1)
    pick = (l_id // two == r_id // heads) & (l_id % heads == r_id % heads)
    diag = lax.broadcasted_iota(jnp.int32, (heads, 128), 1) % heads == lax.broadcasted_iota(jnp.int32, (heads, 128), 0)
    s_id = groups * lax.broadcasted_iota(jnp.int32, (rows, 128), 0) + lax.broadcasted_iota(jnp.int32, (rows, 128), 1) // heads
    zero_q = jnp.zeros((heads, hd), BF16)

    def all_groups(vals, op):
        vals = op(vals, pltpu.roll(vals, heads, 1))
        return op(vals, pltpu.roll(vals, 2 * heads, 1))

    s_list = []
    for tok in range(blk):
        pos = pos_ref[pl.program_id(0) * blk + tok]
        q_tok = q_ref[tok]
        top = jnp.concatenate([q_tok, zero_q], axis=1)
        bot = jnp.concatenate([zero_q, q_tok], axis=1)
        q_mat = jnp.concatenate([top, bot, top, bot], axis=0)
        k_tok = k_ref[tok].reshape(seq // 2, 2, heads, hd)
        k_mat = jnp.concatenate([k_tok[:, 0].reshape(seq // 2 * heads, hd), k_tok[:, 1].reshape(seq // 2 * heads, hd)], axis=1)
        raw = lax.dot_general(k_mat, q_mat, (((1,), (1,)), ((), ())), preferred_element_type=F32)
        s_tok = jnp.sum(jnp.where(pick[None], raw.reshape(rows, two, 128), 0.0), axis=1) * scale
        s_list.append(jnp.where(s_id < pos, s_tok, -jnp.inf)[None])
    s_cache = jnp.concatenate(s_list, axis=0)
    new_col = jnp.sum(q_ref[...].astype(F32) * kn_ref[...].astype(F32), axis=2, keepdims=True)
    s_new = jnp.sum(jnp.where(diag[None], new_col, 0.0), axis=1) * scale
    top_val = jnp.maximum(all_groups(jnp.max(s_cache, axis=1), jnp.maximum), s_new)
    e_cache = jnp.exp(s_cache - top_val[:, None, :])
    e_new = jnp.exp(s_new - top_val)
    denom = all_groups(jnp.sum(e_cache, axis=1), jnp.add) + e_new
    p_cache = e_cache / denom[:, None, :]
    p_new = (e_new / denom).astype(BF16).astype(F32)
    lane_id = lax.broadcasted_iota(jnp.int32, (heads, 128), 1)
    once = diag & (lane_id < heads)
    p_col = jnp.sum(jnp.where(once[None], p_new[:, None, :], 0.0), axis=2, keepdims=True)
    for tok in range(blk):
        p_rows = [jnp.where(diag, p_cache[tok, r:r + 1, :], 0.0).astype(BF16) for r in range(rows)]
        p_mat = jnp.concatenate([jnp.concatenate(p_rows[:half], axis=1), jnp.concatenate(p_rows[half:], axis=1)], axis=0)
        v_tok = v_ref[tok].reshape(2, seq // 2 * heads, hd)
        v_mat = jnp.concatenate([v_tok[0], v_tok[1]], axis=1)
        vals = jnp.dot(p_mat, v_mat, preferred_element_type=F32)
        o_ref[tok] = vals[:heads, :hd] + vals[heads:, hd:] + p_col[tok] * vn_ref[tok].astype(F32)


def attend(positions, q_rot, key_new, value_new, k_cache, v_cache):
    toks, seq, heads, hd = k_cache.shape
    blk = 8
    row = pl.BlockSpec((blk, heads, hd), lambda i, pos: (i, 0, 0))
    cache = pl.BlockSpec((blk, seq, heads, hd), lambda i, pos: (i, 0, 0, 0))
    return pl.pallas_call(
        attend_kernel,
        grid_spec=pltpu.PrefetchScalarGridSpec(
            num_scalar_prefetch=1, grid=(toks // blk,),
            in_specs=[row, row, row, cache, cache], out_specs=row),
        out_shape=jax.ShapeDtypeStruct((toks, heads, hd), F32),
        compiler_params=pltpu.CompilerParams(dimension_semantics=("arbitrary",), vmem_limit_bytes=VMEM_CAP),
        cost_estimate=pl.CostEstimate(flops=4 * toks * seq * heads * hd * 32, bytes_accessed=4 * toks * seq * heads * hd, transcendentals=0),
        name="attend",
    )(positions, q_rot, key_new, value_new, k_cache, v_cache)


def out_kernel(heads, x_ref, a_ref, w_ref, vec_ref, wr_ref, route_ref, x1_out, h2_out, g_out, a_scr):
    step = pl.program_id(0)
    toks = x_ref.shape[0]
    hd = a_ref.shape[1]
    tile = w_ref.shape[1]
    experts = wr_ref.shape[0]

    @pl.when(step == 0)
    def _():
        for head in range(heads):
            a_scr[:, head * hd:(head + 1) * hd] = a_ref[pl.ds(head, toks, stride=heads), :].astype(BF16)

    cols = pl.ds(pl.multiple_of(step * tile, tile), tile)
    lin = jnp.dot(a_scr[...], w_ref[...], preferred_element_type=F32)
    x1_out[:, cols] = (x_ref[:, cols].astype(F32) + lin + vec_ref[5:6, cols]).astype(BF16)

    @pl.when(step == pl.num_programs(0) - 1)
    def _():
        h_two = layer_norm(x1_out[...].astype(F32), vec_ref[6:7, :], vec_ref[7:8, :]).astype(BF16)
        h2_out[...] = h_two
        logits = lax.dot_general(wr_ref[...], h_two, (((1,), (1,)), ((), ())), preferred_element_type=F32)
        ids = lax.broadcasted_iota(jnp.int32, logits.shape, 0)
        hit_one, hit_two = ids == route_ref[0:1, :], ids == route_ref[1:2, :]
        keep_one = route_ref[8:8 + experts, :] == 1
        keep_two = keep_one & jnp.logical_not(hit_one)

        def prob(keep):
            masked = jnp.where(keep, logits, -jnp.inf)
            expd = jnp.exp(masked - jnp.max(masked, axis=0, keepdims=True))
            return expd / jnp.sum(expd, axis=0, keepdims=True)

        g_out[...] = jnp.where(hit_one, prob(keep_one), 0.0) + jnp.where(hit_two, prob(keep_two), 0.0)


def out_project(tokens, attn, w_out, vecs, w_router_t, routes):
    toks, d_model = tokens.shape
    rows, hd = attn.shape
    tile = 512
    experts = w_router_t.shape[0]
    return pl.pallas_call(
        functools.partial(out_kernel, rows // toks),
        grid=(d_model // tile,),
        in_specs=[full_spec((toks, d_model)), full_spec((rows, hd)), pl.BlockSpec((w_out.shape[0], tile), lambda i: (0, i)),
                  full_spec(vecs.shape), full_spec((experts, d_model)), full_spec(routes.shape)],
        out_specs=[full_spec((toks, d_model)), full_spec((toks, d_model)), full_spec((experts, toks))],
        out_shape=[jax.ShapeDtypeStruct((toks, d_model), BF16), jax.ShapeDtypeStruct((toks, d_model), BF16),
                   jax.ShapeDtypeStruct((experts, toks), F32)],
        scratch_shapes=[pltpu.VMEM((toks, w_out.shape[0]), BF16)],
        compiler_params=pltpu.CompilerParams(dimension_semantics=("arbitrary",), vmem_limit_bytes=VMEM_CAP),
        cost_estimate=pl.CostEstimate(flops=2 * toks * d_model * d_model, bytes_accessed=2 * d_model * d_model, transcendentals=0),
        name="out_project",
    )(tokens, attn, w_out, vecs, w_router_t, routes)


def peer(me, flip):
    for bit in (1, 2, 4):
        if flip & bit:
            me = me + bit - 2 * bit * lax.rem(me // bit, 2)
    return me


PIECE = {(0, 0): 0, (0, 1): 1, (1, 0): 2, (1, 1): 3,
         (2, 0): 4, (4, 1): 5, (3, 0): 6, (5, 1): 7,
         (2, 1): 8, (4, 0): 9, (3, 1): 10, (5, 0): 11,
         (6, 0): 12, (6, 1): 13, (7, 0): 14, (7, 1): 15}


def moe_kernel(h_ref, gate_ref, x_ref, wg_hbm, wu_hbm, wd_hbm, out_ref,
               wg, wu, wd, hbuf, gates, wcol, zt_scr, z_scr, mine, first, dsend, drecv, yrecv, local_sem, send_sem, recv_sem):
    me = lax.axis_index('ep')
    toks, d_model = h_ref.shape
    ff = wg.shape[0]
    part = toks // 2
    parts = 4

    own = pltpu.make_async_copy(h_ref, hbuf.at[pl.ds(0, toks)], local_sem.at[0])
    own.start()
    loads = []
    for hbm, scr in ((wg_hbm, wg), (wu_hbm, wu), (wd_hbm, wd)):
        size = ff // 2
        for piece in range(2):
            rows = pl.ds(piece * size, size)
            loads.append(pltpu.make_async_copy(hbm.at[rows], scr.at[rows], local_sem.at[1 + len(loads)]))

    barrier = pltpu.get_barrier_semaphore()
    for flip in range(1, 8):
        pl.semaphore_signal(barrier, inc=1, device_id=(peer(me, flip),), device_id_type=pl.DeviceIdType.MESH)
    pl.semaphore_wait(barrier, 7)

    def remote(num, src, dst, flip):
        return pltpu.make_async_remote_copy(src_ref=src, dst_ref=dst, send_sem=send_sem.at[num], recv_sem=recv_sem.at[num],
                                            device_id=(peer(me, flip),), device_id_type=pl.DeviceIdType.MESH)

    def piece(flip, half):
        return hbuf.at[pl.ds(PIECE[(flip, half)] * part, part)]

    def pass_on(num, source, half, flip):
        return remote(num, piece(source, half), piece(source ^ flip, half), flip)

    sends = {}
    for num, half, flip in ((0, 0, 2), (3, 1, 4), (1, 1, 2), (2, 0, 4)):
        sends[num] = pass_on(num, 0, half, flip)
    sends[4] = remote(4, hbuf.at[pl.ds(0, toks)], hbuf.at[pl.ds(toks, toks)], 1)
    for num, source, half, flip in ((5, 2, 0, 4), (6, 4, 1, 2), (7, 2, 0, 1), (8, 2, 1, 1), (9, 4, 0, 1), (10, 4, 1, 1), (11, 6, 0, 1), (12, 6, 1, 1)):
        sends[num] = pass_on(num, source, half, flip)
    for flip in range(1, 8):
        sends[12 + flip] = remote(12 + flip, gate_ref, gates.at[flip], flip)
    for blk in range(4):
        sends[20 + blk] = remote(20 + blk, dsend.at[blk % 2], drecv.at[blk], 1)
    lower, upper = pl.ds(0, part), pl.ds(part, part)
    sends[24] = remote(24, drecv.at[1, lower], yrecv.at[0, lower], 2)
    sends[25] = remote(25, drecv.at[1, upper], yrecv.at[1, upper], 4)
    sends[26] = remote(26, drecv.at[2, lower], yrecv.at[0, upper], 2)
    sends[27] = remote(27, drecv.at[2, upper], yrecv.at[1, lower], 4)
    sends[28] = remote(28, drecv.at[3], yrecv.at[2], 6)

    own.wait()
    for num in (0, 3, 1, 2, 4):
        sends[num].start()
    for flip in range(1, 8):
        sends[12 + flip].start()
    for load in loads:
        load.start()
    gates[0] = gate_ref[...]
    for flip in range(1, 8):
        sends[12 + flip].wait_recv()
    same = lax.broadcasted_iota(jnp.int32, (toks, toks), 0) == lax.broadcasted_iota(jnp.int32, (toks, toks), 1)
    for flip in range(8):
        col = jnp.sum(jnp.where(same, gates[flip, pl.ds(me, 1), :], 0.0), axis=1, keepdims=True)
        for half in range(2):
            wcol[pl.ds(PIECE[(flip, half)] * part, part), :] = col[half * part:(half + 1) * part]

    def hidden(blk):
        size = ff // 2

        @pl.loop(0, 2)
        def _(idx):
            rows = pl.ds(pl.multiple_of(idx * size, 16), size)
            h_blk = hbuf[pl.ds(blk * 2 * toks, 2 * toks), :]
            nt = (((1,), (1,)), ((), ()))
            u_val = lax.dot_general(wg[rows, :], h_blk, nt, preferred_element_type=F32)
            v_val = lax.dot_general(wu[rows, :], h_blk, nt, preferred_element_type=F32)
            zt_scr[rows, :] = jax.nn.silu(u_val) * v_val

        z_scr[...] = zt_scr[...].T.astype(BF16)

    tile = 512

    def down(blk, first_row, store):
        rows = pl.ds(blk * 2 * toks + first_row, toks)

        @pl.loop(0, d_model // tile)
        def _(idx):
            cols = pl.ds(pl.multiple_of(idx * tile, tile), tile)
            val = jnp.dot(z_scr[pl.ds(first_row, toks), :], wd[:, cols], preferred_element_type=F32).astype(BF16)
            store(cols, wcol[rows, :] * val.astype(F32))

    def keep_theirs(blk):
        def store(cols, val):
            dsend[blk % 2, :, cols] = val.astype(BF16)
        return store

    def keep_mine(cols, val):
        mine[:, cols] = val

    def merge(blk):
        @pl.loop(0, d_model // tile)
        def _(idx):
            cols = pl.ds(pl.multiple_of(idx * tile, tile), tile)
            total = mine[:, cols] + drecv[blk, :, cols].astype(F32)
            if blk == 0:
                first[:, cols] = total
            else:
                drecv[blk, :, cols] = total.astype(BF16)

    def forward(arrived, nums):
        for num in arrived:
            sends[num].wait_recv()
        for num in nums:
            sends[num].start()

    forward((0, 3), (5, 6, 7, 10))
    for load in loads:
        load.wait()
    sends[4].wait_recv()
    homeward = {0: (), 1: (24, 25), 2: (26, 27), 3: (28,)}
    needs = {0: (), 1: (7, 10), 2: (8, 9), 3: (11, 12)}
    for blk in range(4):
        for num in needs[blk]:
            sends[num].wait_recv()
        hidden(blk)
        if blk == 0:
            forward((1, 2), (8, 9))
        if blk == 2:
            forward((5, 6), (11, 12))
        if blk >= 2:
            sends[18 + blk].wait_send()
        down(blk, toks, keep_theirs(blk))
        sends[20 + blk].start()
        down(blk, 0, keep_mine)
        sends[20 + blk].wait_recv()
        merge(blk)
        for num in homeward[blk]:
            sends[num].start()

    for num in range(24, 29):
        sends[num].wait_recv()

    @pl.loop(0, d_model // tile)
    def _(idx):
        cols = pl.ds(pl.multiple_of(idx * tile, tile), tile)
        total = first[:, cols] + yrecv[0, :, cols].astype(F32) + yrecv[1, :, cols].astype(F32) + yrecv[2, :, cols].astype(F32)
        out_ref[:, cols] = (x_ref[:, cols].astype(F32) + total).astype(BF16)

    for num in list(range(20)) + list(range(22, 29)):
        sends[num].wait_send()


def expert_exchange(h_two, gates, x_mid, w_gate_t, w_up_t, w_down):
    toks, d_model = h_two.shape
    ff = w_down.shape[0]
    experts = gates.shape[0]
    hbm = pl.BlockSpec(memory_space=pl.ANY)
    vmem = pl.BlockSpec(memory_space=pltpu.VMEM)
    return pl.pallas_call(
        moe_kernel,
        in_specs=[hbm, vmem, vmem, hbm, hbm, hbm],
        out_specs=vmem,
        out_shape=jax.ShapeDtypeStruct((toks, d_model), BF16),
        scratch_shapes=[
            pltpu.VMEM((ff, d_model), BF16), pltpu.VMEM((ff, d_model), BF16), pltpu.VMEM((ff, d_model), BF16),
            pltpu.VMEM((8 * toks, d_model), BF16),
            pltpu.VMEM((8, experts, toks), F32),
            pltpu.VMEM((8 * toks, 1), F32),
            pltpu.VMEM((ff, 2 * toks), F32),
            pltpu.VMEM((2 * toks, ff), BF16),
            pltpu.VMEM((toks, d_model), F32),
            pltpu.VMEM((toks, d_model), F32),
            pltpu.VMEM((2, toks, d_model), BF16),
            pltpu.VMEM((4, toks, d_model), BF16),
            pltpu.VMEM((3, toks, d_model), BF16),
            pltpu.SemaphoreType.DMA((7,)),
            pltpu.SemaphoreType.DMA((29,)),
            pltpu.SemaphoreType.DMA((29,)),
        ],
        compiler_params=pltpu.CompilerParams(collective_id=0, has_side_effects=True, vmem_limit_bytes=67043328),
        cost_estimate=pl.CostEstimate(flops=48 * toks * d_model * ff, bytes_accessed=6 * d_model * ff, transcendentals=0),
        name="expert_exchange",
    )(h_two, gates, x_mid, w_gate_t, w_up_t, w_down)


def solution(mesh):
    def local_step(tokens, k_cache, v_cache, positions, expert_one, expert_two, eligible, ln1_gain, ln1_bias, w_query, b_query, w_key, b_key, w_value, b_value, w_out, b_out, ln2_gain, ln2_bias, w_router, w_gate, w_up, w_down):
        toks, seq, heads, hd = k_cache.shape
        cos_tab, sin_tab = rope_tables(positions, hd)
        vecs = jnp.concatenate([ln1_gain, ln1_bias, b_query, b_key, b_value, b_out, ln2_gain, ln2_bias]).reshape(8, -1).astype(F32)
        pad = jnp.zeros((6, toks), jnp.int32)
        routes = jnp.concatenate([expert_one[None], expert_two[None], pad, eligible.T], axis=0)
        q_rot, key_new, value_new = (v.reshape(toks, heads, hd) for v in qkv_project(tokens, vecs, cos_tab, sin_tab, w_query, w_key, w_value))
        attn = attend(positions, q_rot, key_new, value_new, k_cache, v_cache)
        x_mid, h_two, gates = out_project(tokens, attn.reshape(toks * heads, hd), w_out, vecs, w_router.T, routes)
        tokens_out = expert_exchange(h_two, gates, x_mid, w_gate[0].T, w_up[0].T, w_down[0])
        return tokens_out, key_new, value_new

    row_spec = P('ep', None)
    cache_spec = P('ep', None, None, None)
    vec_spec = P('ep')
    rep_one = P(None)
    rep_two = P(None, None)
    expert_spec = P('ep', None, None)
    in_specs = (row_spec, cache_spec, cache_spec, vec_spec, vec_spec, vec_spec, row_spec, rep_one, rep_one, rep_two, rep_one, rep_two, rep_one, rep_two, rep_one, rep_two, rep_one, rep_one, rep_one, rep_two, expert_spec, expert_spec, expert_spec)
    out_specs = (row_spec, expert_spec, expert_spec)
    return jax.shard_map(local_step, mesh=mesh, in_specs=in_specs, out_specs=out_specs, check_vma=False)
```

time: 368 us -> 232 us (0.63)
  waiting for transfers between devices: 97.2 us -> 0 us
  Pallas kernels: 163 us -> 219 us
  matrix products: 52.6 us -> 0 us
  blocking collectives: 18.5 us -> 0 us
  between operations: 14.1 us -> 0.65 us
  local copies, waits for them, and re-layouts: 16.8 us -> 8.62 us
    pallas_call x0 -> x1, Pallas kernels: none -> 111 us  [expert_exchange(): pl.pallas_call(moe_kernel, in_specs=[hbm, vmem, vmem, hbm, hbm, hbm], out...]
    reduce_scatter x1 -> x0, waiting for transfers between devices: 62.4 us -> none  [local_step(): y_sum = lax.psum_scatter(part, 'ep', scatter_dimension=0, tiled=True)]
    dot_general x3 -> x0, matrix products: 52.6 us -> none  [the longest x1 18.4 us: expert_mlp(): v_val = jnp.dot(expert_in, w_up, preferred_element_type=F32)]
    pallas_call x1, Pallas kernels: 99.2 us -> 52.3 us  [attend(): pl.pallas_call(attend_kernel, grid_spec=pltpu.PrefetchScalarGridSpec(num_...]
    all_gather x1 -> x0, waiting for transfers between devices: 34.8 us -> none  [local_step(): h_all = lax.all_gather(h_two, 'ep', axis=0, tiled=True)]
    all_gather x1 -> x0, blocking collectives: 18.5 us -> none  [local_step(): gates_all = lax.all_gather(gates, 'ep', axis=0, tiled=True)]
    reshape x8 -> x0, local copies, waits for them, and re-layouts: 10.4 us -> none  [the longest x5 6.53 us: qkv_project(): row = lambda v: v.reshape(1, -1)]
    pallas_call x1, Pallas kernels: 23.7 us -> 18.6 us  [out_project(): pl.pallas_call(functools.partial(out_kernel, rows // toks), grid=(d_model...]
  transfers between devices with their start and end apart: 2 -> 0, of which waited for: 2 -> 0; matrix products, arithmetic and copies ran while one was open for 0% -> 0% of each run, Pallas kernels for 0% -> 0%
where the time goes in v2:
time: 232 us; the launch traced here: 231 us
  Pallas kernels  219 us (94%)
  local copies, waits for them, and re-layouts  8.62 us (4%)
  other arithmetic  3.1 us (1%)
    pallas_call x1, Pallas kernels, expert_exchange(): pl.pallas_call(moe_kernel, in_specs=[hbm, vmem, vmem, hbm, hbm, hbm], out...  111 us
    pallas_call x1, Pallas kernels, attend(): pl.pallas_call(attend_kernel, grid_spec=pltpu.PrefetchScalarGridSpec(num_...  52.3 us
    pallas_call x1, Pallas kernels, qkv_project(): pl.pallas_call(functools.partial(qkv_kernel, heads), grid=(wq.shape[1] //...  36.9 us
    pallas_call x1, Pallas kernels, out_project(): pl.pallas_call(functools.partial(out_kernel, rows // toks), grid=(d_model...  18.6 us
    unnamed x8, local copies, waits for them, and re-layouts  7.17 us

profile of v2, /device:TPU:0, one launch (start us, length us, event | category | flops | bytes accessed | tf_op | source)
XLA Modules:
  0.0 230.9 jit_solution(17616098897160470774)
XLA Ops:
  0.6 0.7 convert_element_type.10
  1.3 0.1 pad.2.clone
  1.4 1.4 pad_add_fusion.route_ref
  2.8 0.7 constant_dynamic-update-slice_fusion.7
  3.5 0.7 constant_dynamic-update-slice_fusion.6
  4.2 0.7 constant_dynamic-update-slice_fusion.5
  4.8 0.7 constant_dynamic-update-slice_fusion.4
  5.5 0.7 constant_dynamic-update-slice_fusion.3
  6.2 0.7 constant_dynamic-update-slice_fusion.2
  6.9 0.7 constant_dynamic-update-slice_fusion.1
  7.6 0.7 constant_dynamic-update-slice_fusion
  8.3 0.7 reshape.31.vec_ref
  9.0 0.3 fusion
  9.3 0.8 pad_maximum_fusion
  10.1 36.9 %qkv_project.1 = (bf16[4096,128]{1,0:T(8,128)(2,1)}, bf16[4096,128]{1,0:T(8,128)(2,1)}, bf16[4096,128]{1,0:T(8,128)(2,1)}) custom-call(bf16[128,4096]{1,0:T(8,128)(2,1)} %x_ref.3, f32[8,4096]{1,0:T(8,128)} %reshape.31.vec_ref, f32[128,128]{1,0:T(8,128)} %get-tuple-element.18.cos_ref, f32[128,128]{1,0:T(8,128)} %get-tuple-element.19.sin_ref, ...), custom_call_target="tpu_custom_call" | custom-call | flops 12884901888 | bytes 100663296 | tf_op jit(solution)/shard_map/qkv_project/pallas_call | solution.py:70
  47.0 52.3 %attend.1 = f32[128,32,128]{2,1,0:T(8,128)} custom-call(s32[128]{0:T(128)} %pos_ref.1, bf16[128,32,128]{2,1,0:T(8,128)(2,1)} %bitcast.20, bf16[128,32,128]{2,1,0:T(8,128)(2,1)} %bitcast.16, bf16[128,32,128]{2,1,0:T(8,128)(2,1)} %bitcast.18, bf16[128,64,32,128]{3,2,1,0:T(8,128)(2,1)} %k_ref.1, bf16[128,64,32,128]{3,2,1,0:T(8,128)(2,1)} %v_ref.1), custom_call_target="tpu_custom_call" | custom-call | flops 4294967296 | bytes 134217728 | tf_op jit(solution)/shard_map/attend/pallas_call | solution.py:139
  99.4 18.6 %out_project.1 = (bf16[128,4096]{1,0:T(8,128)(2,1)}, bf16[128,4096]{1,0:T(8,128)(2,1)}, f32[8,128]{1,0:T(8,128)}) custom-call(bf16[128,4096]{1,0:T(8,128)(2,1)} %x_ref.3, f32[4096,128]{1,0:T(8,128)} %bitcast.15, bf16[4096,4096]{1,0:T(8,128)(2,1)} %w_ref.1, f32[8,4096]{1,0:T(8,128)} %reshape.31.vec_ref, bf16[8,4096]{1,0:T(8,128)(2,1)} %bitcast.21, ...), custom_call_target="tpu_custom_call" | custom-call | flops 4294967296 | bytes 33554432 | tf_op jit(solution)/shard_map/out_project/pallas_call | solution.py:190
  118.0 110.7 %expert_exchange.1 = bf16[128,4096]{1,0:T(8,128)(2,1)} custom-call(bf16[128,4096]{1,0:T(8,128)(2,1)} %get-tuple-element.12.h_ref, f32[8,128]{1,0:T(8,128)} %get-tuple-element.13.gate_ref, bf16[128,4096]{1,0:T(8,128)(2,1)} %get-tuple-element.14.x_ref, bf16[1376,4096]{1,0:T(8,128)(2,1)} %bitcast.25, bf16[1376,4096]{1,0:T(8,128)(2,1)} %bitcast.26, ...), custom_call_target="tpu_custom_call" | custom-call | flops 34628173824 | bytes 33816576 | tf_op jit(solution)/shard_map/expert_exchange/pallas_call | solution.py:375
  228.7 2.3 copy.34
  (2 shorter events, 0.0 us)

commit v3 on v2

--- a/solution.py
+++ b/solution.py
@@ -29,21 +29,58 @@
     return jnp.concatenate([cos_half, cos_half], axis=-1), jnp.concatenate([-sin_half, sin_half], axis=-1)
 
 
-def qkv_kernel(heads, x_ref, vec_ref, cos_ref, sin_ref, wq_ref, wk_ref, wv_ref, q_out, k_out, v_out, h_scr, q_scr, k_scr, v_scr):
+def ring(step, steps, depth, copies):
+    @pl.when(step == 0)
+    def _():
+        for idx in range(depth - 1):
+            for copy in copies(idx):
+                copy.start()
+
+    @pl.when(step + depth - 1 < steps)
+    def _():
+        for copy in copies(step + depth - 1):
+            copy.start()
+
+    for copy in copies(step):
+        copy.wait()
+
+
+def column_copies(hbms, bufs, sems, tile, depth):
+    def copies(idx):
+        slot = lax.rem(idx, depth) if not isinstance(idx, int) else idx % depth
+        start = pl.multiple_of(idx * tile, tile) if not isinstance(idx, int) else idx * tile
+        return [pltpu.make_async_copy(hbm.at[:, pl.ds(start, tile)], buf.at[slot], sems.at[num, slot])
+                for num, (hbm, buf) in enumerate(zip(hbms, bufs))]
+    return copies
+
+
+def as_row(dst, row, vec_ref):
+    width = vec_ref.shape[1]
+    vals = vec_ref[...].astype(F32)
+    for idx in range(vec_ref.shape[0]):
+        dst[row:row + 1, idx * width:(idx + 1) * width] = vals[idx:idx + 1, :]
+
+
+def qkv_kernel(heads, x_ref, g_ref, b_ref, bq_ref, bk_ref, bv_ref, cos_ref, sin_ref, wq_hbm, wk_hbm, wv_hbm, q_out, k_out, v_out,
+               h_scr, q_scr, k_scr, v_scr, vec_ref, wq_buf, wk_buf, wv_buf, sems):
     step = pl.program_id(0)
     toks = x_ref.shape[0]
     hd = cos_ref.shape[1]
-    tile = wq_ref.shape[1]
+    depth, _, tile = wq_buf.shape
+    slot = lax.rem(step, depth)
+    ring(step, pl.num_programs(0), depth, column_copies((wq_hbm, wk_hbm, wv_hbm), (wq_buf, wk_buf, wv_buf), sems, tile, depth))
 
     @pl.when(step == 0)
     def _():
+        for row, ref in enumerate((g_ref, b_ref, bq_ref, bk_ref, bv_ref)):
+            as_row(vec_ref, row, ref)
         h_scr[...] = layer_norm(x_ref[...].astype(F32), vec_ref[0:1, :], vec_ref[1:2, :]).astype(BF16)
 
     h_one = h_scr[...]
     cols = pl.ds(pl.multiple_of(step * tile, tile), tile)
     per_step = tile // hd
-    for row, w_ref, scr in ((2, wq_ref, q_scr), (3, wk_ref, k_scr), (4, wv_ref, v_scr)):
-        lin = jnp.dot(h_one, w_ref[...], preferred_element_type=F32) + vec_ref[row:row + 1, cols]
+    for row, w_buf, scr in ((2, wq_buf, q_scr), (3, wk_buf, k_scr), (4, wv_buf, v_scr)):
+        lin = jnp.dot(h_one, w_buf[slot], preferred_element_type=F32) + vec_ref[row:row + 1, cols]
         for sub in range(per_step):
             part = lin[:, sub * hd:(sub + 1) * hd]
             if row < 4:
@@ -60,28 +97,38 @@
     return pl.BlockSpec(shape, lambda *ids: (0,) * len(shape))
 
 
-def qkv_project(tokens, vecs, cos_tab, sin_tab, wq, wk, wv):
+def qkv_project(tokens, rows, cos_tab, sin_tab, wq, wk, wv):
     toks, d_model = tokens.shape
     hd = cos_tab.shape[1]
     heads = wq.shape[1] // hd
-    tile = 512
-    w_spec = pl.BlockSpec((d_model, tile), lambda i: (0, i))
+    tile, depth = 256, 4
+    w_spec = pl.BlockSpec(memory_space=pl.ANY)
     out = jax.ShapeDtypeStruct((toks * heads, hd), BF16)
     return pl.pallas_call(
         functools.partial(qkv_kernel, heads),
         grid=(wq.shape[1] // tile,),
-        in_specs=[full_spec((toks, d_model)), full_spec(vecs.shape), full_spec((toks, hd)), full_spec((toks, hd)), w_spec, w_spec, w_spec],
+        in_specs=[full_spec((toks, d_model))] + [full_spec(row.shape) for row in rows] + [full_spec((toks, hd)), full_spec((toks, hd)), w_spec, w_spec, w_spec],
         out_specs=[full_spec((toks * heads, hd))] * 3,
         out_shape=[out] * 3,
-        scratch_shapes=[pltpu.VMEM((toks, d_model), BF16)] + [pltpu.VMEM((toks * heads, hd), F32)] * 3,
+        scratch_shapes=[pltpu.VMEM((toks, d_model), BF16)] + [pltpu.VMEM((toks * heads, hd), F32)] * 3
+        + [pltpu.VMEM((8, d_model), F32)] + [pltpu.VMEM((depth, d_model, tile), BF16)] * 3 + [pltpu.SemaphoreType.DMA((3, depth))],
         compiler_params=pltpu.CompilerParams(dimension_semantics=("arbitrary",), vmem_limit_bytes=VMEM_CAP),
         cost_estimate=pl.CostEstimate(flops=6 * toks * d_model * wq.shape[1], bytes_accessed=6 * d_model * wq.shape[1], transcendentals=0),
         name="qkv_project",
-    )(tokens, vecs, cos_tab, sin_tab, wq, wk, wv)
-
-
-def attend_kernel(pos_ref, q_ref, kn_ref, vn_ref, k_ref, v_ref, o_ref):
-    blk, seq, heads, hd = k_ref.shape
+    )(tokens, *rows, cos_tab, sin_tab, wq, wk, wv)
+
+
+def attend_kernel(pos_ref, q_ref, kn_ref, vn_ref, k_hbm, v_hbm, o_ref, k_buf, v_buf, sems):
+    depth, blk, seq, heads, hd = k_buf.shape
+    step = pl.program_id(0)
+
+    def copies(idx):
+        slot = lax.rem(idx, depth) if not isinstance(idx, int) else idx % depth
+        return [pltpu.make_async_copy(hbm.at[pl.ds(idx * blk, blk)], buf.at[slot], sems.at[num, slot])
+                for num, (hbm, buf) in enumerate(((k_hbm, k_buf), (v_hbm, v_buf)))]
+
+    ring(step, pl.num_programs(0), depth, copies)
+    k_ref, v_ref = k_buf.at[lax.rem(step, depth)], v_buf.at[lax.rem(step, depth)]
     groups = 128 // heads
     scale = hd ** -0.5
     rows = seq // groups
@@ -133,14 +180,16 @@
 
 def attend(positions, q_rot, key_new, value_new, k_cache, v_cache):
     toks, seq, heads, hd = k_cache.shape
-    blk = 8
+    blk, depth = 8, 3
     row = pl.BlockSpec((blk, heads, hd), lambda i, pos: (i, 0, 0))
-    cache = pl.BlockSpec((blk, seq, heads, hd), lambda i, pos: (i, 0, 0, 0))
+    cache = pl.BlockSpec(memory_space=pl.ANY)
+    ring_buf = pltpu.VMEM((depth, blk, seq, heads, hd), BF16)
     return pl.pallas_call(
         attend_kernel,
         grid_spec=pltpu.PrefetchScalarGridSpec(
             num_scalar_prefetch=1, grid=(toks // blk,),
-            in_specs=[row, row, row, cache, cache], out_specs=row),
+            in_specs=[row, row, row, cache, cache], out_specs=row,
+            scratch_shapes=[ring_buf, ring_buf, pltpu.SemaphoreType.DMA((2, depth))]),
         out_shape=jax.ShapeDtypeStruct((toks, heads, hd), F32),
         compiler_params=pltpu.CompilerParams(dimension_semantics=("arbitrary",), vmem_limit_bytes=VMEM_CAP),
         cost_estimate=pl.CostEstimate(flops=4 * toks * seq * heads * hd * 32, bytes_accessed=4 * toks * seq * heads * hd, transcendentals=0),
@@ -148,30 +197,33 @@
     )(positions, q_rot, key_new, value_new, k_cache, v_cache)
 
 
-def out_kernel(heads, x_ref, a_ref, w_ref, vec_ref, wr_ref, route_ref, x1_out, h2_out, g_out, a_scr):
+def out_kernel(heads, x_ref, a_ref, w_hbm, bo_ref, g_ref, b_ref, wr_ref, e1_ref, e2_ref, el_ref, x1_out, h2_out, g_out, a_scr, vec_ref, w_buf, sems):
     step = pl.program_id(0)
     toks = x_ref.shape[0]
     hd = a_ref.shape[1]
-    tile = w_ref.shape[1]
+    depth, _, tile = w_buf.shape
     experts = wr_ref.shape[0]
+    ring(step, pl.num_programs(0), depth, column_copies((w_hbm,), (w_buf,), sems, tile, depth))
 
     @pl.when(step == 0)
     def _():
+        for row, ref in enumerate((bo_ref, g_ref, b_ref)):
+            as_row(vec_ref, row, ref)
         for head in range(heads):
             a_scr[:, head * hd:(head + 1) * hd] = a_ref[pl.ds(head, toks, stride=heads), :].astype(BF16)
 
     cols = pl.ds(pl.multiple_of(step * tile, tile), tile)
-    lin = jnp.dot(a_scr[...], w_ref[...], preferred_element_type=F32)
-    x1_out[:, cols] = (x_ref[:, cols].astype(F32) + lin + vec_ref[5:6, cols]).astype(BF16)
+    lin = jnp.dot(a_scr[...], w_buf[lax.rem(step, depth)], preferred_element_type=F32)
+    x1_out[:, cols] = (x_ref[:, cols].astype(F32) + lin + vec_ref[0:1, cols]).astype(BF16)
 
     @pl.when(step == pl.num_programs(0) - 1)
     def _():
-        h_two = layer_norm(x1_out[...].astype(F32), vec_ref[6:7, :], vec_ref[7:8, :]).astype(BF16)
+        h_two = layer_norm(x1_out[...].astype(F32), vec_ref[1:2, :], vec_ref[2:3, :]).astype(BF16)
         h2_out[...] = h_two
         logits = lax.dot_general(wr_ref[...], h_two, (((1,), (1,)), ((), ())), preferred_element_type=F32)
         ids = lax.broadcasted_iota(jnp.int32, logits.shape, 0)
-        hit_one, hit_two = ids == route_ref[0:1, :], ids == route_ref[1:2, :]
-        keep_one = route_ref[8:8 + experts, :] == 1
+        hit_one, hit_two = ids == e1_ref[...], ids == e2_ref[...]
+        keep_one = el_ref[...] == 1
         keep_two = keep_one & jnp.logical_not(hit_one)
 
         def prob(keep):
@@ -182,24 +234,25 @@
         g_out[...] = jnp.where(hit_one, prob(keep_one), 0.0) + jnp.where(hit_two, prob(keep_two), 0.0)
 
 
-def out_project(tokens, attn, w_out, vecs, w_router_t, routes):
+def out_project(tokens, attn, w_out, vec_rows, w_router_t, routes):
     toks, d_model = tokens.shape
     rows, hd = attn.shape
-    tile = 512
+    tile, depth = 256, 6
     experts = w_router_t.shape[0]
     return pl.pallas_call(
         functools.partial(out_kernel, rows // toks),
         grid=(d_model // tile,),
-        in_specs=[full_spec((toks, d_model)), full_spec((rows, hd)), pl.BlockSpec((w_out.shape[0], tile), lambda i: (0, i)),
-                  full_spec(vecs.shape), full_spec((experts, d_model)), full_spec(routes.shape)],
+        in_specs=[full_spec((toks, d_model)), full_spec((rows, hd)), pl.BlockSpec(memory_space=pl.ANY)]
+        + [full_spec(row.shape) for row in vec_rows] + [full_spec((experts, d_model))] + [full_spec(route.shape) for route in routes],
         out_specs=[full_spec((toks, d_model)), full_spec((toks, d_model)), full_spec((experts, toks))],
         out_shape=[jax.ShapeDtypeStruct((toks, d_model), BF16), jax.ShapeDtypeStruct((toks, d_model), BF16),
                    jax.ShapeDtypeStruct((experts, toks), F32)],
-        scratch_shapes=[pltpu.VMEM((toks, w_out.shape[0]), BF16)],
+        scratch_shapes=[pltpu.VMEM((toks, w_out.shape[0]), BF16), pltpu.VMEM((8, d_model), F32),
+                        pltpu.VMEM((depth, w_out.shape[0], tile), BF16), pltpu.SemaphoreType.DMA((1, depth))],
         compiler_params=pltpu.CompilerParams(dimension_semantics=("arbitrary",), vmem_limit_bytes=VMEM_CAP),
         cost_estimate=pl.CostEstimate(flops=2 * toks * d_model * d_model, bytes_accessed=2 * d_model * d_model, transcendentals=0),
         name="out_project",
-    )(tokens, attn, w_out, vecs, w_router_t, routes)
+    )(tokens, attn, w_out, *vec_rows, w_router_t, *routes)
 
 
 def peer(me, flip):
@@ -255,17 +308,19 @@
         sends[num] = pass_on(num, source, half, flip)
     for flip in range(1, 8):
         sends[12 + flip] = remote(12 + flip, gate_ref, gates.at[flip], flip)
-    for blk in range(4):
-        sends[20 + blk] = remote(20 + blk, dsend.at[blk % 2], drecv.at[blk], 1)
+    order = (0, 3, 1, 2)
+    for turn, blk in enumerate(order):
+        sends[20 + blk] = remote(20 + blk, dsend.at[turn % 2], drecv.at[blk], 1)
     lower, upper = pl.ds(0, part), pl.ds(part, part)
     sends[24] = remote(24, drecv.at[1, lower], yrecv.at[0, lower], 2)
     sends[25] = remote(25, drecv.at[1, upper], yrecv.at[1, upper], 4)
     sends[26] = remote(26, drecv.at[2, lower], yrecv.at[0, upper], 2)
     sends[27] = remote(27, drecv.at[2, upper], yrecv.at[1, lower], 4)
-    sends[28] = remote(28, drecv.at[3], yrecv.at[2], 6)
+    sends[28] = remote(28, drecv.at[3, lower], yrecv.at[2, upper], 2)
+    sends[29] = remote(29, drecv.at[3, upper], yrecv.at[2, lower], 4)
 
     own.wait()
-    for num in (0, 3, 1, 2, 4):
+    for num in (0, 3, 4):
         sends[num].start()
     for flip in range(1, 8):
         sends[12 + flip].start()
@@ -305,9 +360,9 @@
             val = jnp.dot(z_scr[pl.ds(first_row, toks), :], wd[:, cols], preferred_element_type=F32).astype(BF16)
             store(cols, wcol[rows, :] * val.astype(F32))
 
-    def keep_theirs(blk):
+    def keep_theirs(turn):
         def store(cols, val):
-            dsend[blk % 2, :, cols] = val.astype(BF16)
+            dsend[turn % 2, :, cols] = val.astype(BF16)
         return store
 
     def keep_mine(cols, val):
@@ -318,6 +373,8 @@
         def _(idx):
             cols = pl.ds(pl.multiple_of(idx * tile, tile), tile)
             total = mine[:, cols] + drecv[blk, :, cols].astype(F32)
+            if blk == 2:
+                total = total + yrecv[2, :, cols].astype(F32)
             if blk == 0:
                 first[:, cols] = total
             else:
@@ -329,40 +386,43 @@
         for num in nums:
             sends[num].start()
 
-    forward((0, 3), (5, 6, 7, 10))
+    forward((0, 3), (5, 6, 7, 10, 1, 2))
     for load in loads:
         load.wait()
     sends[4].wait_recv()
-    homeward = {0: (), 1: (24, 25), 2: (26, 27), 3: (28,)}
-    needs = {0: (), 1: (7, 10), 2: (8, 9), 3: (11, 12)}
-    for blk in range(4):
+    homeward = {0: (), 3: (28, 29), 1: (24, 25), 2: (26, 27)}
+    needs = {0: (), 3: (11, 12), 1: (7, 10), 2: (8, 9)}
+    for turn, blk in enumerate(order):
         for num in needs[blk]:
             sends[num].wait_recv()
         hidden(blk)
-        if blk == 0:
-            forward((1, 2), (8, 9))
-        if blk == 2:
-            forward((5, 6), (11, 12))
-        if blk >= 2:
-            sends[18 + blk].wait_send()
-        down(blk, toks, keep_theirs(blk))
+        if turn >= 2:
+            sends[20 + order[turn - 2]].wait_send()
+        down(blk, toks, keep_theirs(turn))
         sends[20 + blk].start()
         down(blk, 0, keep_mine)
+        if blk == 0:
+            forward((5, 6), (11, 12))
         sends[20 + blk].wait_recv()
+        if blk == 2:
+            for num in (28, 29):
+                sends[num].wait_recv()
         merge(blk)
         for num in homeward[blk]:
             sends[num].start()
-
-    for num in range(24, 29):
+        if blk == 3:
+            forward((1, 2), (8, 9))
+
+    for num in range(24, 28):
         sends[num].wait_recv()
 
     @pl.loop(0, d_model // tile)
     def _(idx):
         cols = pl.ds(pl.multiple_of(idx * tile, tile), tile)
-        total = first[:, cols] + yrecv[0, :, cols].astype(F32) + yrecv[1, :, cols].astype(F32) + yrecv[2, :, cols].astype(F32)
+        total = first[:, cols] + yrecv[0, :, cols].astype(F32) + yrecv[1, :, cols].astype(F32)
         out_ref[:, cols] = (x_ref[:, cols].astype(F32) + total).astype(BF16)
 
-    for num in list(range(20)) + list(range(22, 29)):
+    for num in list(range(20)) + [21, 22] + list(range(24, 30)):
         sends[num].wait_send()
 
 
@@ -390,8 +450,8 @@
             pltpu.VMEM((4, toks, d_model), BF16),
             pltpu.VMEM((3, toks, d_model), BF16),
             pltpu.SemaphoreType.DMA((7,)),
-            pltpu.SemaphoreType.DMA((29,)),
-            pltpu.SemaphoreType.DMA((29,)),
+            pltpu.SemaphoreType.DMA((30,)),
+            pltpu.SemaphoreType.DMA((30,)),
         ],
         compiler_params=pltpu.CompilerParams(collective_id=0, has_side_effects=True, vmem_limit_bytes=67043328),
         cost_estimate=pl.CostEstimate(flops=48 * toks * d_model * ff, bytes_accessed=6 * d_model * ff, transcendentals=0),
@@ -403,12 +463,11 @@
     def local_step(tokens, k_cache, v_cache, positions, expert_one, expert_two, eligible, ln1_gain, ln1_bias, w_query, b_query, w_key, b_key, w_value, b_value, w_out, b_out, ln2_gain, ln2_bias, w_router, w_gate, w_up, w_down):
         toks, seq, heads, hd = k_cache.shape
         cos_tab, sin_tab = rope_tables(positions, hd)
-        vecs = jnp.concatenate([ln1_gain, ln1_bias, b_query, b_key, b_value, b_out, ln2_gain, ln2_bias]).reshape(8, -1).astype(F32)
-        pad = jnp.zeros((6, toks), jnp.int32)
-        routes = jnp.concatenate([expert_one[None], expert_two[None], pad, eligible.T], axis=0)
-        q_rot, key_new, value_new = (v.reshape(toks, heads, hd) for v in qkv_project(tokens, vecs, cos_tab, sin_tab, w_query, w_key, w_value))
+        lanes = lambda vec: vec.reshape(-1, 128)
+        routes = (expert_one.reshape(1, toks), expert_two.reshape(1, toks), eligible.T)
+        q_rot, key_new, value_new = (v.reshape(toks, heads, hd) for v in qkv_project(tokens, tuple(map(lanes, (ln1_gain, ln1_bias, b_query, b_key, b_value))), cos_tab, sin_tab, w_query, w_key, w_value))
         attn = attend(positions, q_rot, key_new, value_new, k_cache, v_cache)
-        x_mid, h_two, gates = out_project(tokens, attn.reshape(toks * heads, hd), w_out, vecs, w_router.T, routes)
+        x_mid, h_two, gates = out_project(tokens, attn.reshape(toks * heads, hd), w_out, tuple(map(lanes, (b_out, ln2_gain, ln2_bias))), w_router.T, routes)
         tokens_out = expert_exchange(h_two, gates, x_mid, w_gate[0].T, w_up[0].T, w_down[0])
         return tokens_out, key_new, value_new
 

time: 232 us -> 192 us (0.83)
  Pallas kernels: 219 us -> 187 us
  local copies, waits for them, and re-layouts: 8.62 us -> 2.29 us
    pallas_call x1, Pallas kernels: 111 us -> 90.1 us  [expert_exchange(): pl.pallas_call(moe_kernel, in_specs=[hbm, vmem, vmem, hbm, hbm, hbm], out...]
    pallas_call x1, Pallas kernels: 52.3 us -> 45.5 us  [attend(): pl.pallas_call(attend_kernel, grid_spec=pltpu.PrefetchScalarGridSpec(num_...]
    unnamed x8 -> x1, local copies, waits for them, and re-layouts: 7.17 us -> 2.29 us
    pallas_call x1, Pallas kernels: 18.6 us -> 16 us  [out_project(): pl.pallas_call(functools.partial(out_kernel, rows // toks), grid=(d_model...]
where the time goes in v3:
time: 192 us
  Pallas kernels  187 us (97%)
  local copies, waits for them, and re-layouts  2.29 us (1%)
    pallas_call x1, Pallas kernels, expert_exchange(): pl.pallas_call(moe_kernel, in_specs=[hbm, vmem, vmem, hbm, hbm, hbm], out...  90.1 us
    pallas_call x1, Pallas kernels, attend(): pl.pallas_call(attend_kernel, grid_spec=pltpu.PrefetchScalarGridSpec(num_...  45.5 us
    pallas_call x1, Pallas kernels, qkv_project(): pl.pallas_call(functools.partial(qkv_kernel, heads), grid=(wq.shape[1] //...  35.3 us
    pallas_call x1, Pallas kernels, out_project(): pl.pallas_call(functools.partial(out_kernel, rows // toks), grid=(d_model...  16 us

profile of v3, /device:TPU:0, one launch (start us, length us, event | category | flops | bytes accessed | tf_op | source)
XLA Modules:
  0.0 191.6 jit_solution(8220649049440375776)
XLA Ops:
  0.6 0.7 convert_element_type.3
  1.3 0.3 fusion
  1.6 0.8 pad_maximum_fusion
  2.4 35.3 %qkv_project.1 = (bf16[4096,128]{1,0:T(8,128)(2,1)}, bf16[4096,128]{1,0:T(8,128)(2,1)}, bf16[4096,128]{1,0:T(8,128)(2,1)}) custom-call(bf16[128,4096]{1,0:T(8,128)(2,1)} %x_ref.3, bf16[32,128]{1,0:T(8,128)(2,1)} %bitcast.30, bf16[32,128]{1,0:T(8,128)(2,1)} %bitcast.31, bf16[32,128]{1,0:T(8,128)(2,1)} %bitcast.32, bf16[32,128]{1,0:T(8,128)(2,1)} %bitcast.33, ...), custom_call_target="tpu_custom_call" | custom-call | flops 12884901888 | bytes 100663296 | tf_op jit(solution)/shard_map/qkv_project/pallas_call | solution.py:107
  37.7 45.5 %attend.1 = f32[128,32,128]{2,1,0:T(8,128)} custom-call(s32[128]{0:T(128)} %pos_ref.1, bf16[128,32,128]{2,1,0:T(8,128)(2,1)} %bitcast.28, bf16[128,32,128]{2,1,0:T(8,128)(2,1)} %bitcast.24, bf16[128,32,128]{2,1,0:T(8,128)(2,1)} %bitcast.26, bf16[128,64,32,128]{3,2,1,0:T(8,128)(2,1)} %k_hbm.1, bf16[128,64,32,128]{3,2,1,0:T(8,128)(2,1)} %v_hbm.1), custom_call_target="tpu_custom_call" | custom-call | flops 4294967296 | bytes 134217728 | tf_op jit(solution)/shard_map/attend/pallas_call | solution.py:187
  83.3 16.0 %out_project.1 = (bf16[128,4096]{1,0:T(8,128)(2,1)}, bf16[128,4096]{1,0:T(8,128)(2,1)}, f32[8,128]{1,0:T(8,128)}) custom-call(bf16[128,4096]{1,0:T(8,128)(2,1)} %x_ref.3, f32[4096,128]{1,0:T(8,128)} %bitcast.23, bf16[4096,4096]{1,0:T(8,128)(2,1)} %w_hbm.1, bf16[32,128]{1,0:T(8,128)(2,1)} %bitcast.35, bf16[32,128]{1,0:T(8,128)(2,1)} %bitcast.36, ...), custom_call_target="tpu_custom_call" | custom-call | flops 4294967296 | bytes 33554432 | tf_op jit(solution)/shard_map/out_project/pallas_call | solution.py:242
  99.2 90.1 %expert_exchange.1 = bf16[128,4096]{1,0:T(8,128)(2,1)} custom-call(bf16[128,4096]{1,0:T(8,128)(2,1)} %get-tuple-element.12.h_ref, f32[8,128]{1,0:T(8,128)} %get-tuple-element.13.gate_ref, bf16[128,4096]{1,0:T(8,128)(2,1)} %get-tuple-element.14.x_ref, bf16[1376,4096]{1,0:T(8,128)(2,1)} %bitcast.41, bf16[1376,4096]{1,0:T(8,128)(2,1)} %bitcast.42, ...), custom_call_target="tpu_custom_call" | custom-call | flops 34628173824 | bytes 33816576 | tf_op jit(solution)/shard_map/expert_exchange/pallas_call | solution.py:435
  189.3 2.3 %copy.27 = bf16[128,4096]{1,0:T(8,128)(2,1)} copy(bf16[128,4096]{1,0:T(8,128)(2,1)} %expert_exchange.1) | data formatting | bytes 2097152
  (1 shorter events, 0.0 us)

commit v4 on v3

--- a/solution.py
+++ b/solution.py
@@ -180,7 +180,7 @@
 
 def attend(positions, q_rot, key_new, value_new, k_cache, v_cache):
     toks, seq, heads, hd = k_cache.shape
-    blk, depth = 8, 3
+    blk, depth = 4, 5
     row = pl.BlockSpec((blk, heads, hd), lambda i, pos: (i, 0, 0))
     cache = pl.BlockSpec(memory_space=pl.ANY)
     ring_buf = pltpu.VMEM((depth, blk, seq, heads, hd), BF16)
@@ -324,7 +324,9 @@
         sends[num].start()
     for flip in range(1, 8):
         sends[12 + flip].start()
-    for load in loads:
+    early = (loads[0], loads[2])
+    late = (loads[1], loads[3], loads[4], loads[5])
+    for load in early:
         load.start()
     gates[0] = gate_ref[...]
     for flip in range(1, 8):
@@ -335,10 +337,10 @@
         for half in range(2):
             wcol[pl.ds(PIECE[(flip, half)] * part, part), :] = col[half * part:(half + 1) * part]
 
-    def hidden(blk):
+    def hidden(blk, first_trip=0, last_trip=2):
         size = ff // 2
 
-        @pl.loop(0, 2)
+        @pl.loop(first_trip, last_trip)
         def _(idx):
             rows = pl.ds(pl.multiple_of(idx * size, 16), size)
             h_blk = hbuf[pl.ds(blk * 2 * toks, 2 * toks), :]
@@ -347,7 +349,8 @@
             v_val = lax.dot_general(wu[rows, :], h_blk, nt, preferred_element_type=F32)
             zt_scr[rows, :] = jax.nn.silu(u_val) * v_val
 
-        z_scr[...] = zt_scr[...].T.astype(BF16)
+        if last_trip == 2:
+            z_scr[...] = zt_scr[...].T.astype(BF16)
 
     tile = 512
 
@@ -386,16 +389,21 @@
         for num in nums:
             sends[num].start()
 
+    for load in early:
+        load.wait()
+    for load in late:
+        load.start()
+    sends[4].wait_recv()
+    hidden(0, 0, 1)
     forward((0, 3), (5, 6, 7, 10, 1, 2))
-    for load in loads:
+    for load in late:
         load.wait()
-    sends[4].wait_recv()
     homeward = {0: (), 3: (28, 29), 1: (24, 25), 2: (26, 27)}
     needs = {0: (), 3: (11, 12), 1: (7, 10), 2: (8, 9)}
     for turn, blk in enumerate(order):
         for num in needs[blk]:
             sends[num].wait_recv()
-        hidden(blk)
+        hidden(blk, 1 if blk == 0 else 0)
         if turn >= 2:
             sends[20 + order[turn - 2]].wait_send()
         down(blk, toks, keep_theirs(turn))

time: 192 us -> 205 us (1.068)
  Pallas kernels: 187 us -> 200 us
    pallas_call x1, Pallas kernels: 45.5 us -> 55 us  [attend(): pl.pallas_call(attend_kernel, grid_spec=pltpu.PrefetchScalarGridSpec(num_...]
    pallas_call x1, Pallas kernels: 90.1 us -> 93.7 us  [expert_exchange(): pl.pallas_call(moe_kernel, in_specs=[hbm, vmem, vmem, hbm, hbm, hbm], out...]
where the time goes in v4:
time: 205 us
  Pallas kernels  200 us (98%)
  local copies, waits for them, and re-layouts  2.29 us (1%)
    pallas_call x1, Pallas kernels, expert_exchange(): pl.pallas_call(moe_kernel, in_specs=[hbm, vmem, vmem, hbm, hbm, hbm], out...  93.7 us
    pallas_call x1, Pallas kernels, attend(): pl.pallas_call(attend_kernel, grid_spec=pltpu.PrefetchScalarGridSpec(num_...  55 us
    pallas_call x1, Pallas kernels, qkv_project(): pl.pallas_call(functools.partial(qkv_kernel, heads), grid=(wq.shape[1] //...  35.3 us
    pallas_call x1, Pallas kernels, out_project(): pl.pallas_call(functools.partial(out_kernel, rows // toks), grid=(d_model...  16 us

profile of v4, /device:TPU:0, one launch (start us, length us, event | category | flops | bytes accessed | tf_op | source)
XLA Modules:
  0.0 204.7 jit_solution(18410758782540046987)
XLA Ops:
  0.6 0.7 convert_element_type.3
  1.3 0.3 fusion
  1.6 0.8 pad_maximum_fusion
  2.4 35.3 %qkv_project.1 = (bf16[4096,128]{1,0:T(8,128)(2,1)}, bf16[4096,128]{1,0:T(8,128)(2,1)}, bf16[4096,128]{1,0:T(8,128)(2,1)}) custom-call(bf16[128,4096]{1,0:T(8,128)(2,1)} %x_ref.3, bf16[32,128]{1,0:T(8,128)(2,1)} %bitcast.30, bf16[32,128]{1,0:T(8,128)(2,1)} %bitcast.31, bf16[32,128]{1,0:T(8,128)(2,1)} %bitcast.32, bf16[32,128]{1,0:T(8,128)(2,1)} %bitcast.33, ...), custom_call_target="tpu_custom_call" | custom-call | flops 12884901888 | bytes 100663296 | tf_op jit(solution)/shard_map/qkv_project/pallas_call | solution.py:107
  37.7 55.0 %attend.1 = f32[128,32,128]{2,1,0:T(8,128)} custom-call(s32[128]{0:T(128)} %pos_ref.1, bf16[128,32,128]{2,1,0:T(8,128)(2,1)} %bitcast.28, bf16[128,32,128]{2,1,0:T(8,128)(2,1)} %bitcast.24, bf16[128,32,128]{2,1,0:T(8,128)(2,1)} %bitcast.26, bf16[128,64,32,128]{3,2,1,0:T(8,128)(2,1)} %k_hbm.1, bf16[128,64,32,128]{3,2,1,0:T(8,128)(2,1)} %v_hbm.1), custom_call_target="tpu_custom_call" | custom-call | flops 4294967296 | bytes 134217728 | tf_op jit(solution)/shard_map/attend/pallas_call | solution.py:187
  92.8 16.0 %out_project.1 = (bf16[128,4096]{1,0:T(8,128)(2,1)}, bf16[128,4096]{1,0:T(8,128)(2,1)}, f32[8,128]{1,0:T(8,128)}) custom-call(bf16[128,4096]{1,0:T(8,128)(2,1)} %x_ref.3, f32[4096,128]{1,0:T(8,128)} %bitcast.23, bf16[4096,4096]{1,0:T(8,128)(2,1)} %w_hbm.1, bf16[32,128]{1,0:T(8,128)(2,1)} %bitcast.35, bf16[32,128]{1,0:T(8,128)(2,1)} %bitcast.36, ...), custom_call_target="tpu_custom_call" | custom-call | flops 4294967296 | bytes 33554432 | tf_op jit(solution)/shard_map/out_project/pallas_call | solution.py:242
  108.7 93.7 %expert_exchange.1 = bf16[128,4096]{1,0:T(8,128)(2,1)} custom-call(bf16[128,4096]{1,0:T(8,128)(2,1)} %get-tuple-element.12.h_ref, f32[8,128]{1,0:T(8,128)} %get-tuple-element.13.gate_ref, bf16[128,4096]{1,0:T(8,128)(2,1)} %get-tuple-element.14.x_ref, bf16[1376,4096]{1,0:T(8,128)(2,1)} %bitcast.41, bf16[1376,4096]{1,0:T(8,128)(2,1)} %bitcast.42, ...), custom_call_target="tpu_custom_call" | custom-call | flops 34628173824 | bytes 33816576 | tf_op jit(solution)/shard_map/expert_exchange/pallas_call | solution.py:443
  202.4 2.3 %copy.27 = bf16[128,4096]{1,0:T(8,128)(2,1)} copy(bf16[128,4096]{1,0:T(8,128)(2,1)} %expert_exchange.1) | data formatting | bytes 2097152
  (1 shorter events, 0.0 us)
